TPU v7x, 512 devices: a whole 4x8x8 slice. The times are simulated.
512 devices in a mesh: seq: 32 (over y, x), dp: 16 (over z, core).
Axes of the slice: x: 4, y: 8, z: 8, core: 2. Of those that a mesh axis runs over, the one named last changes fastest.
Arguments:
- layer_input: bfloat16 [16, 8192, 2560], P('dp', 'seq'), may hold values from -14400 to 14400
- scan_input: bfloat16 [16, 8192, 2560], P('dp', 'seq'), may hold values from -0.75 to 0.75
- scan_cotangent: bfloat16 [16, 8192, 2560], P('dp', 'seq'), may hold values from -0.03125 to 0.03125
- step_size: float32 [16, 40, 8192], P('dp', None, 'seq'), may hold values from 0.5 to 2
- log_decay: float32 [16, 40, 8192], P('dp', None, 'seq'), may hold values from -2.25 to 0
- state_inputs: bfloat16 [16, 8192, 256], P('dp', 'seq'), may hold values from -4 to 4
- entry_state: bfloat16 [16, 32, 2560, 128], P('dp', 'seq'), may hold values from -8 to 8
Outputs:
- state_input_grad: bfloat16 [16, 8192, 256], P('dp', 'seq')
- weight_grad: float32 [2560, 256], P(('seq', 'dp'))
All inputs are finite; a program needn't handle non-finite values. Where the computation divides by a largest or mean magnitude, that divisor is 1e-20 or more.
Results may differ from a plain program's by a relative error of at most 0.013.
Values may be sent and summed in bfloat16 or wider, within the bound.
A program may use at most 128 MiB of HBM per device.

v0:
```python
import functools

import jax
import jax.numpy as jnp
from jax import lax
from jax.sharding import Mesh
from jax.sharding import PartitionSpec as P

STRETCH = 256
SEQ_DP = ("seq_0", "seq_1", "dp_0", "dp_1")
SEQ = ("seq_0", "seq_1")
DP = ("dp_0", "dp_1")


epsilon = 1e-06


def by_axis(x, axes):
    return functools.reduce(lax.pmax, axes, x)


def filled_with(x, identity):
    return jax.tree.map(
        lambda part, zero: jnp.zeros_like(part) + jnp.asarray(zero, part.dtype), x, identity
    )


def prefix_by_axis(x, axes, combine, identity):
    before = start = filled_with(x, identity)
    running = x
    for axis in reversed(axes):
        length, place = (lax.axis_size(axis), lax.axis_index(axis))
        pieces = jax.tree.map(
            lambda part, kind: lax.all_gather(part.astype(kind), axis),
            running,
            (jnp.bfloat16, jnp.bfloat16),
        )
        inside, running = (start, start)
        for k in reversed(range(length)):
            passed = k > place
            running = combine(
                running, jax.tree.map(lambda part, own: part[k].astype(own.dtype), pieces, x)
            )
            inside = jax.tree.map(lambda new, old: jnp.where(passed, new, old), running, inside)
        before = combine(inside, before)
    return before


def in_blocks(x, dim, length):
    lengths = x.shape
    tiles = x.reshape(*lengths[:dim], length, lengths[dim] // length, *lengths[dim + 1 :])
    return jnp.moveaxis(tiles, dim, 0)


def sent_and_summed(x, axis, dim):
    tiles = in_blocks(x, dim, lax.axis_size(axis))
    arrived = lax.all_to_all(tiles, axis, split_axis=0, concat_axis=0, tiled=True)
    return arrived.astype(jnp.float32).sum(axis=0)


def summed_on_arrival(x, axis, dim):
    length = lax.axis_size(axis)
    tiles = lax.all_to_all(in_blocks(x, dim, length), axis, 0, 0, tiled=True)
    return jnp.sum(tiles, axis=0)


def silu_slope(value):
    sigma = jax.nn.sigmoid(value)
    return sigma * (1.0 + value * (1.0 - sigma))


def compose(earlier, later):
    return (earlier[0] * later[0], later[1] + later[0][:, :, None, None] * earlier[1])


def block_summary(pieces):
    inputs, cotangents, steps, cumulative, writes, reads = pieces
    weighted_cot = (cotangents * jnp.exp(cumulative).T[:, :, None]).astype(jnp.bfloat16)
    weighted_in = (
        inputs * (steps * jnp.exp(cumulative[:, -1:] - cumulative)).T[:, :, None]
    ).astype(jnp.bfloat16)
    from_later = jnp.einsum("thp,tn->hpn", weighted_cot, reads, preferred_element_type=jnp.float32)
    from_earlier = jnp.einsum(
        "thp,tn->hpn", weighted_in, writes, preferred_element_type=jnp.float32
    )
    return (weighted_cot, weighted_in, from_later, from_earlier, jnp.exp(cumulative[:, -1]))


def block_inner(pieces):
    inputs, cotangents, steps, cumulative, writes, reads = pieces
    length = inputs.shape[0]
    later = lax.broadcasted_iota(jnp.int32, (length, length), 0) >= lax.broadcasted_iota(
        jnp.int32, (length, length), 1
    )
    scores = jnp.einsum("shp,thp->hst", cotangents, inputs, preferred_element_type=jnp.float32)
    spread = jnp.where(later[None], cumulative[:, :, None] - cumulative[:, None, :], 0.0)
    decay = jnp.where(later[None], jnp.exp(spread), 0.0)
    mixing = (scores * decay * steps[:, None, :]).astype(jnp.bfloat16)
    inner_write = jnp.einsum("hst,sn->tn", mixing, reads, preferred_element_type=jnp.float32)
    inner_read = jnp.einsum("hst,tn->sn", mixing, writes, preferred_element_type=jnp.float32)
    return (inner_write, inner_read)


def block_both(pieces):
    return block_summary(pieces) + block_inner(pieces)


def on_device(
    layer_input, scan_input, scan_cotangent, step_size, log_decay, state_inputs, entry_state
):
    seq_local, tokens, width = layer_input.shape
    heads = step_size.shape[1]
    channels = scan_input.shape[2]
    head_size = channels // heads
    states = state_inputs.shape[2] // 2
    blocks = tokens // STRETCH
    count = seq_local * blocks
    local_peaks = jnp.max(jnp.abs(layer_input), axis=(0, 1))
    peaks = by_axis(local_peaks, SEQ_DP).astype(jnp.float32)
    inputs = scan_input.reshape(count, STRETCH, heads, head_size)
    cotangents = scan_cotangent.reshape(count, STRETCH, heads, head_size)
    steps = (
        step_size.reshape(seq_local, heads, blocks, STRETCH)
        .transpose(0, 2, 1, 3)
        .reshape(count, heads, STRETCH)
    )
    decays = (
        log_decay.reshape(seq_local, heads, blocks, STRETCH)
        .transpose(0, 2, 1, 3)
        .reshape(count, heads, STRETCH)
    )
    cumulative = jnp.cumsum(decays, axis=2)
    preact = state_inputs.astype(jnp.float32)
    activated = jax.nn.silu(preact).astype(jnp.bfloat16)
    writes = activated[:, :, :states]
    reads = activated[:, :, states:]
    pieces = (inputs, cotangents, steps, cumulative, writes, reads)
    weighted_cot, weighted_in, from_later, from_earlier, totals, inner_write, inner_read = lax.map(
        block_both, pieces
    )
    from_later = from_later.reshape(seq_local, blocks, heads, head_size, states)
    from_earlier = from_earlier.reshape(seq_local, blocks, heads, head_size, states)
    totals = totals.reshape(seq_local, blocks, heads)
    later_sum = from_later[:, blocks - 1]
    device_decay = jnp.prod(totals, axis=1)
    identity = (jnp.ones_like(device_decay), jnp.zeros_like(later_sum))
    beyond = prefix_by_axis((device_decay, later_sum), SEQ, compose, identity)[1]
    weighted_in = weighted_in.reshape(seq_local, blocks, STRETCH, channels)
    weighted_cot = weighted_cot.reshape(seq_local, blocks, STRETCH, channels)
    carried_write = []
    state_now = beyond
    block_index = 0
    operand = state_now.astype(jnp.bfloat16).reshape(seq_local, channels, states)
    carried_write.append(
        jnp.einsum(
            "btk,bkn->btn", weighted_in[:, block_index], operand, preferred_element_type=jnp.float32
        )
    )
    carried_write = jnp.stack(carried_write[::-1], axis=1).reshape(seq_local, tokens, states)
    carried_read = []
    state_now = entry_state.reshape(seq_local, heads, head_size, states).astype(jnp.float32)
    block_index = 0
    operand = state_now.astype(jnp.bfloat16).reshape(seq_local, channels, states)
    carried_read.append(
        jnp.einsum(
            "btk,bkn->btn",
            weighted_cot[:, block_index],
            operand,
            preferred_element_type=jnp.float32,
        )
    )
    carried_read = jnp.stack(carried_read, axis=1).reshape(seq_local, tokens, states)
    grad_write = inner_write + carried_write
    grad_read = inner_read + carried_read
    state_input_grad = (
        jnp.concatenate([grad_write, grad_read], axis=2) * silu_slope(preact)
    ).astype(jnp.bfloat16)
    factor = 1.0 / (peaks + epsilon)
    quantized = (layer_input.reshape(seq_local * tokens, width) * factor).astype(jnp.bfloat16)
    grads = state_input_grad.reshape(seq_local * tokens, 2 * states)
    partial_rows = sent_and_summed(
        lax.dot_general(
            quantized, grads, (((0,), (0,)), ((), ())), preferred_element_type=jnp.float32
        ).astype(jnp.bfloat16),
        SEQ,
        0,
    )
    summed = summed_on_arrival(partial_rows, DP, 0)
    return (state_input_grad, summed)


def solution(mesh):
    torus = Mesh(mesh.devices.reshape(8, 4, 8, 2), ("seq_0", "seq_1", "dp_0", "dp_1"))
    placed = (
        P(DP, SEQ, None),
        P(DP, SEQ, None),
        P(DP, SEQ, None),
        P(DP, None, SEQ),
        P(DP, None, SEQ),
        P(DP, SEQ, None),
        P(DP, SEQ, None, None),
    )
    return jax.shard_map(
        on_device,
        mesh=torus,
        in_specs=placed,
        out_specs=(P(DP, SEQ, None), P(SEQ_DP, None)),
        check_vma=False,
    )
```

profile of v0, /device:TPU:1, one launch (start us, length us, event | category | flops | bytes accessed | tf_op | source)
XLA Modules:
  0.0 214.3 jit_solution(10862501995342099276)
XLA Ops:
  7.2 0.0 copy-start
  7.2 0.0 all-gather.7.cloned.1.call-start
  7.2 0.8 copy_bitcast_fusion
  8.1 0.6 reduce-window.6
  8.6 0.2 slice_reduce_fusion
  8.9 0.1 copy.33
  9.0 1.0 copy.34
  10.0 0.1 fusion.36
  10.1 1.6 copy.29
  11.7 0.0 copy-start.2
  11.7 0.1 broadcast.284
  11.8 0.8 exponential_bitcast_fusion
  12.6 0.3 fusion
  12.9 0.0 copy-done.2
  12.9 0.0 copy-start.7
  12.9 1.4 convolution_convert_fusion.1
  14.3 0.0 all-gather.7.cloned.1.call-update
  14.3 0.0 all-gather.5.cloned.1.call-start
  14.4 1.3 dynamic-slice
  16.3 0.0 copy-done.7
  16.3 0.2 fusion.48
  16.5 0.2 dynamic-update-slice
  16.7 9.3 %all-reduce = bf16[160]{0:T(256)(128)(2,1)S(1)} all-reduce(bf16[160]{0:T(256)(128)(2,1)S(1)} %dynamic-update-slice), channel_id=3, replica_groups=mesh['seq_0'=8,'seq_1'=4,'dp_0'=8,'dp_1'=2] {'seq_1'}, use_global_device_ids=true, to_apply=%add | all-reduce | flops 160 | bytes 640
  26.0 0.6 broadcast_select_fusion.3
  26.6 0.6 slice_convert_fusion.3
  27.2 33.0 %all-gather.7.cloned.1.call-done = bf16[160,64,128]{2,1,0:T(8,128)(2,1)} async-done(((bf16[40,64,128]{2,1,0:T(8,128)(2,1)}), bf16[160,64,128]{2,1,0:T(8,128)(2,1)}) %all-gather.7.cloned.1.call-update) | async-done | bytes 2621456 | tf_op jit(solution)/shard_map/all_gather | solution.py:34
  60.2 3.4 %fusion.19 = bf16[1,1,40,64,128]{4,3,2,1,0:T(8,128)(2,1)} fusion(f32[40]{0:T(128)S(1)} %get-tuple-element.59, f32[40]{0:T(128)} %get-tuple-element.60, f32[40]{0:T(128)S(1)} %get-tuple-element.58, f32[40]{0:T(128)S(1)} %get-tuple-element.57, bf16[160,64,128]{2,1,0:T(8,128)(2,1)} %all-gather.7.cloned.1.call-done), kind=kLoop, calls=%fused_computation.29 | loop fusion | flops 3932160 | bytes 3277440 | tf_op jit(solution)/shard_map/convert_element_type | solution.py:34
  63.6 0.0 copy-done.10
  63.6 0.0 copy-done.12
  63.6 0.0 copy-done.13
  63.6 0.0 all-gather.5.cloned.1.call-update
  63.6 1.4 copy.30
  65.1 0.9 slice_reduce_fusion.1
  66.0 0.9 multiply_bitcast_fusion
  66.9 0.0 copy-start.1
  66.9 2.8 %fusion.1 = bf16[1,256,2560]{1,2,0:T(8,128)(2,1)} fusion(bf16[1,256,2560]{1,2,0:T(8,128)(2,1)} %copy.30, f32[256,40]{0,1:T(8,128)S(1)} %multiply_bitcast_fusion), kind=kLoop, calls=%fused_computation.6 | loop fusion | flops 1966080 | bytes 2662400 | tf_op jit(solution)/shard_map/while/body/eval_jaxpr/convert_element_type | solution.py:81
  69.7 0.1 fusion.59
  69.8 13.3 %all_gather.22 = bf16[8,1,40]{2,1,0:T(2,128)(2,1)} all-gather(bf16[1,1,40]{2,1,0:T(2,128)(2,1)S(1)} %fusion.59), channel_id=1, replica_groups=mesh['seq_0'=8,'seq_1'=4,'dp_0'=8,'dp_1'=2] {'seq_0'}, dimensions={0}, use_global_device_ids=true | all-gather | bytes 720 | tf_op jit(solution)/shard_map/all_gather | solution.py:34
  83.1 0.2 abs_reduce_fusion
  83.2 14.4 %pmax.28 = bf16[2560]{0:T(1024)(128)(2,1)S(1)} all-reduce(bf16[2560]{0:T(1024)(128)(2,1)S(1)} %abs_reduce_fusion), channel_id=1, replica_groups=mesh['seq_0'=8,'seq_1'=4,'dp_0'=8,'dp_1'=2] {'seq_0'}, use_global_device_ids=true, to_apply=%region_4.0 | all-reduce | flops 2560 | bytes 10240 | tf_op jit(solution)/shard_map/pmax | solution.py:19
  97.7 7.1 %pmax.29 = bf16[2560]{0:T(1024)(128)(2,1)S(1)} all-reduce(bf16[2560]{0:T(1024)(128)(2,1)S(1)} %pmax.28), channel_id=1, replica_groups=mesh['seq_0'=8,'seq_1'=4,'dp_0'=8,'dp_1'=2] {'seq_1'}, use_global_device_ids=true, to_apply=%region_5.0 | all-reduce | flops 2560 | bytes 10240 | tf_op jit(solution)/shard_map/pmax | solution.py:19
  104.8 16.2 %pmax.30 = bf16[2560]{0:T(1024)(128)(2,1)S(1)} all-reduce(bf16[2560]{0:T(1024)(128)(2,1)S(1)} %pmax.29), channel_id=1, replica_groups=mesh['seq_0'=8,'seq_1'=4,'dp_0'=8,'dp_1'=2] {'dp_0'}, use_global_device_ids=true, to_apply=%region_6.7 | all-reduce | flops 2560 | bytes 10240 | tf_op jit(solution)/shard_map/pmax | solution.py:19
  121.0 13.7 %pmax.31 = bf16[2560]{0:T(1024)(128)(2,1)} all-reduce(bf16[2560]{0:T(1024)(128)(2,1)S(1)} %pmax.30), channel_id=1, replica_groups=mesh['seq_0'=8,'seq_1'=4,'dp_0'=8,'dp_1'=2] {'dp_1'}, use_global_device_ids=true, to_apply=%region_7.8 | all-reduce | flops 2560 | bytes 10240 | tf_op jit(solution)/shard_map/pmax | solution.py:19
  134.8 5.7 %convert_reduce_fusion = bf16[256,256]{1,0:T(8,128)(2,1)S(1)} fusion(f32[40,256]{1,0:T(8,128)} %bitcast.162, f32[40,256]{1,0:T(8,128)} %get-tuple-element.35, pred[256,256]{1,0:T(8,128)(4,1)S(1)} %iota_compare_fusion, bf16[256,40,64]{0,2,1:T(8,128)(2,1)} %bitcast.156, bf16[256,40,64]{0,2,1:T(8,128)(2,1)} %bitcast.157), kind=kOutput, calls=%fused_computation | convolution fusion | flops 356450304 | bytes 2899968 | tf_op jit(solution)/shard_map/while/body/eval_jaxpr/shp,thp->hst/dot_general | solution.py:95
  140.5 0.0 copy-start.8
  140.6 0.2 fusion.42
  140.8 1.1 fusion.29
  141.8 0.5 fusion.50
  142.4 0.6 fusion.57
  143.0 0.0 copy-done.8
  143.0 0.8 fusion.44
  143.8 6.1 %fusion.11 = bf16[1,1,40,64,128]{4,3,2,1,0:T(8,128)(2,1)S(1)} fusion(bf16[8,1,40,64,128]{4,3,2,1,0:T(8,128)(2,1)} %all-gather.5.cloned.1.call-done, f32[40]{0:T(128)} %copy-done.13, f32[40]{0:T(128)} %get-tuple-element.60, f32[40]{0:T(128)} %copy-done.12, f32[40]{0:T(128)} %fusion.50, f32[40]{0:T(128)} %get-tuple-element.37, f32[40]{0:T(128)} %get-tuple-element.38, ...), kind=kLoop, calls=%fused_computation.19 | loop fusion | flops 16056320 | bytes 8521772 | tf_op jit(solution)/shard_map/convert_element_type | solution.py:153
  149.9 0.0 copy-start.6
  149.9 0.4 fusion.23
  150.4 0.4 copy-done.6
  150.8 0.1 fusion.40
  150.9 0.6 convolution_convert_fusion
  151.5 39.4 %all_to_all.10 = bf16[32,80,256]{2,1,0:T(8,128)(2,1)S(1)} all-to-all(bf16[32,80,256]{2,1,0:T(8,128)(2,1)S(1)} %bitcast.158), channel_id=1, replica_groups=mesh['seq_0'=8,'seq_1'=4,'dp_0'=8,'dp_1'=2] {'seq_0','seq_1'}, dimensions={0} | all-to-all | bytes 2621440 | tf_op jit(solution)/shard_map/all_to_all | solution.py:57
  190.9 0.2 convert_reduce_fusion.1
  191.1 0.7 reshape.515
  191.7 6.2 %all-to-all-start.1 = ((f32[16,5,256]{2,1,0:T(8,128)}), f32[16,5,256]{2,1,0:T(8,128)S(1)}, u32[]{:S(2)}, u32[]{:S(2)}) async-start(f32[16,5,256]{2,1,0:T(8,128)} %reshape.515), calls=%async_computation.1 | async-start | bytes 262144 | tf_op jit(solution)/shard_map/all_to_all | solution.py:63
  197.9 0.8 copy.38
  198.7 8.1 %all-to-all-done.1 = f32[16,5,256]{2,1,0:T(8,128)S(1)} async-done(((f32[16,5,256]{2,1,0:T(8,128)}), f32[16,5,256]{2,1,0:T(8,128)S(1)}, u32[]{:S(2)}, u32[]{:S(2)}) %all-to-all-start.1) | async-done | bytes 81952 | tf_op jit(solution)/shard_map/all_to_all | solution.py:63
  206.8 0.6 reduce_sum.34
  (22 shorter events, 0.1 us)
Async XLA Ops:
  7.2 133.6 %copy-start = (bf16[1,1,2560,128]{3,2,1,0:T(8,128)(2,1)S(1)}, bf16[1,1,2560,128]{3,2,1,0:T(8,128)(2,1)}, u32[]{:S(2)}) copy-start(bf16[1,1,2560,128]{3,2,1,0:T(8,128)(2,1)} %param.13) | copy-start | bytes 1966084
  7.2 53.0 %all-gather.7.cloned.1.call-start = ((), (), s32[]{:S(2)}) async-start(), calls=%async_computation.3 | async-start | bytes 3276800 | tf_op jit(solution)/shard_map/all_gather | solution.py:34
  11.7 1.2 copy-start.2
  12.9 3.4 %copy-start.7 = (f32[40,256]{1,0:T(8,128)S(1)}, f32[40,256]{1,0:T(8,128)}, u32[]{:S(2)}) copy-start(f32[40,256]{1,0:T(8,128)} %get-tuple-element.35) | copy-start | bytes 122884
  14.3 129.5 %all-gather.5.cloned.1.call-start = ((), (), s32[]{:S(2)}) async-start(), calls=%async_computation.2 | async-start | bytes 5898240 | tf_op jit(solution)/shard_map/all_gather | solution.py:34
  26.6 37.0 %copy-start.10 = (f32[40]{0:T(128)}, f32[40]{0:T(128)S(1)}, u32[]{:S(2)}) copy-start(f32[40]{0:T(128)S(1)} %get-tuple-element.57) | copy-start | bytes 484
  27.2 36.4 %copy-start.12 = (f32[40]{0:T(128)}, f32[40]{0:T(128)S(1)}, u32[]{:S(2)}) copy-start(f32[40]{0:T(128)S(1)} %get-tuple-element.58) | copy-start | bytes 484
  27.2 36.4 %copy-start.13 = (f32[40]{0:T(128)}, f32[40]{0:T(128)S(1)}, u32[]{:S(2)}) copy-start(f32[40]{0:T(128)S(1)} %get-tuple-element.59) | copy-start | bytes 484
  60.2 3.4 %copy-start.4 = (bf16[1,256,2560]{2,1,0:T(8,128)(2,1)S(1)}, bf16[1,256,2560]{2,1,0:T(8,128)(2,1)}, u32[]{:S(2)}) copy-start(bf16[1,256,2560]{2,1,0:T(8,128)(2,1)} %param.8) | copy-start | bytes 3932164
  66.9 16.2 %copy-start.1 = (bf16[1,256,2560]{2,1,0:T(8,128)(2,1)S(1)}, bf16[1,256,2560]{2,1,0:T(8,128)(2,1)}, u32[]{:S(2)}) copy-start(bf16[1,256,2560]{2,1,0:T(8,128)(2,1)} %param.7) | copy-start | bytes 3932164
  140.5 1.3 copy-start.9
  140.5 2.4 %copy-start.8 = (bf16[2560]{0:T(1024)(128)(2,1)S(1)}, bf16[2560]{0:T(1024)(128)(2,1)}, u32[]{:S(2)}) copy-start(bf16[2560]{0:T(1024)(128)(2,1)} %pmax.31) | copy-start | bytes 15364
  140.8 3.1 %copy-start.11 = (f32[40]{0:T(128)S(1)}, f32[40]{0:T(128)}, u32[]{:S(2)}) copy-start(f32[40]{0:T(128)} %copy-done.10) | copy-start | bytes 484
  143.8 6.1 %copy-start.3 = (bf16[1,256,2560]{1,2,0:T(8,128)(2,1)S(1)}, bf16[1,256,2560]{1,2,0:T(8,128)(2,1)}, u32[]{:S(2)}) copy-start(bf16[1,256,2560]{1,2,0:T(8,128)(2,1)} %fusion.1) | copy-start | bytes 3932164
  143.8 6.1 %copy-start.5 = (f32[256,128]{0,1:T(8,128)S(1)}, f32[256,128]{0,1:T(8,128)}, u32[]{:S(2)}) copy-start(f32[256,128]{0,1:T(8,128)} %fusion.44) | copy-start | bytes 393220
  149.9 0.9 copy-start.6
  191.7 15.1 %all-to-all-start.1 = ((f32[16,5,256]{2,1,0:T(8,128)}), f32[16,5,256]{2,1,0:T(8,128)S(1)}, u32[]{:S(2)}, u32[]{:S(2)}) async-start(f32[16,5,256]{2,1,0:T(8,128)} %reshape.515), calls=%async_computation.1 | async-start | bytes 262144 | tf_op jit(solution)/shard_map/all_to_all | solution.py:63
Sparse Core Ops, SparseCore 0:
  14.4 45.7 all-gather.6
  63.7 67.7 all-gather.4
where the time goes:
time: 215 us; the launch traced here: 214 us
  blocking collectives  113 us (53%)
  waiting for transfers between devices  41.2 us (19%)
  other arithmetic  18.6 us (9%)
  between operations  15 us (7%)
  matrix products  10.2 us (5%)
  local copies, waits for them, and re-layouts  9.6 us (4%)
  starting transfers between devices  6.31 us (3%)
    pmax x4, blocking collectives, by_axis(): return functools.reduce(lax.pmax, axes, x)  51.5 us
    all_to_all x1, blocking collectives, sent_and_summed(): lax.all_to_all(tiles, axis, split_axis=0, concat_axis=0, tiled=True)  39.4 us
    all_gather x2, waiting for transfers between devices, prefix_by_axis(): lax.all_gather(part.astype(kind), axis)  33 us
    all_gather x1, blocking collectives, prefix_by_axis(): lax.all_gather(part.astype(kind), axis)  13.3 us
    unnamed x1, blocking collectives  9.26 us
    all_to_all x1, waiting for transfers between devices, summed_on_arrival(): tiles = lax.all_to_all(in_blocks(x, dim, length), axis, 0, 0, tiled=True)  8.13 us
    unnamed x35, local copies, waits for them, and re-layouts  6.82 us
    all_to_all x1, starting transfers between devices, summed_on_arrival(): tiles = lax.all_to_all(in_blocks(x, dim, length), axis, 0, 0, tiled=True)  6.23 us
  transfers between devices with their start and end apart: 3, of which 2 were waited for; matrix products, arithmetic and copies ran while one was open for 9% of the time, Pallas kernels for 0%

commit v1 on v0

v1 whole, which is shorter than its diff:
```python
import functools

import jax
import jax.numpy as jnp
from jax import lax
from jax.experimental import pallas as pl
from jax.experimental.pallas import tpu as pltpu
from jax.sharding import Mesh
from jax.sharding import PartitionSpec as P

AXES = ("seq_0", "seq_1", "dp_0", "dp_1")
SEQ = ("seq_0", "seq_1")
DP = ("dp_0", "dp_1")
MESH_ID = pl.DeviceIdType.MESH
F32 = jnp.float32
BF16 = jnp.bfloat16
EPSILON = 1e-06
LANES = 128
FAR = -1.0e9
VMEM_BYTES = 60 * 1024 * 1024


def product(a, b):
    return lax.dot_general(a, b, (((1,), (0,)), ((), ())), preferred_element_type=F32)


def product_nt(a, b):
    return lax.dot_general(a, b, (((1,), (1,)), ((), ())), preferred_element_type=F32)


def split(x, parts):
    pieces = []
    for _ in range(parts):
        piece = x.astype(BF16)
        pieces.append(piece)
        x = x - piece.astype(F32)
    return pieces


def one_hot(heads, width, first, head_size):
    row = lax.broadcasted_iota(jnp.int32, (heads, width), 0)
    lane = lax.broadcasted_iota(jnp.int32, (heads, width), 1) + first
    start = row * head_size
    return jnp.where((lane >= start) & (lane < start + head_size), 1.0, 0.0).astype(BF16)


def send(src, dst, send_sem, recv_sem, where):
    return pltpu.make_async_remote_copy(
        src_ref=src,
        dst_ref=dst,
        send_sem=send_sem,
        recv_sem=recv_sem,
        device_id=where,
        device_id_type=MESH_ID,
    )


def scan_kernel(
    sizes,
    x_hbm, in_hbm, cot_hbm, step_hbm, ld_hbm, si_hbm, es_hbm,
    sig_ref, g_ref, pk_ref,
    xv, inv, cotv, stepv, ldv, siv, esv,
    wc, wi, xt, fl, by, rx1, tot_s, tot_x, tots_y, tot_y, rs, ry1, bs, ry2, bx,
    mm, cum_ref, cs_ref, ei_ref, slope_ref, act_ref,
    in_sem, tot_ss, tot_rs, x1_ss, x1_rs, toty_ss, toty_rs, y1_ss, y1_rs, y2_ss, y2_rs, x2_ss, x2_rs,
):
    ny, nx = sizes
    tokens, width = xv.shape
    channels = inv.shape[1]
    heads = ldv.shape[0]
    head_size = channels // heads
    states = act_ref.shape[1] // 2
    tiles = channels // LANES
    group = tiles // nx
    rows = states // ny
    y = lax.axis_index("seq_0")
    x = lax.axis_index("seq_1")

    arrivals = [
        pltpu.make_async_copy(src, dst, in_sem.at[i])
        for i, (src, dst) in enumerate(
            (
                (ld_hbm, ldv), (step_hbm, stepv), (si_hbm, siv), (cot_hbm, cotv),
                (in_hbm, inv), (x_hbm, xv), (es_hbm, esv),
            )
        )
    ]
    for copy in arrivals:
        copy.start()

    barrier = pltpu.get_barrier_semaphore()
    for d in range(1, nx):
        pl.semaphore_signal(barrier, inc=1, device_id={"seq_1": lax.rem(x + d, nx)}, device_id_type=MESH_ID)
    for d in range(1, ny):
        pl.semaphore_signal(barrier, inc=1, device_id={"seq_0": lax.rem(y + d, ny)}, device_id_type=MESH_ID)

    for copy in arrivals[:3]:
        copy.wait()
    upper = (
        lax.broadcasted_iota(jnp.int32, (tokens, tokens), 0)
        <= lax.broadcasted_iota(jnp.int32, (tokens, tokens), 1)
    )
    ones = jnp.where(upper, 1.0, 0.0).astype(BF16)
    cum = functools.reduce(jnp.add, [product(p, ones) for p in reversed(split(ldv[...], 3))])
    last = cum[:, tokens - 1 : tokens]
    cum_ref[...] = cum
    cs_ref[:, 0:heads] = cum.T
    ei_ref[...] = stepv[...] * jnp.exp(last - cum)
    factor = jnp.exp(cum).T
    factor_parts = split(factor, 2)
    preact = siv[...].astype(F32)
    sigma = 1.0 / (1.0 + jnp.exp(-preact))
    act = preact * sigma
    slope_ref[...] = sigma * (1.0 + preact * (1.0 - sigma))
    act_ref[...] = act.astype(BF16)
    reads_t = act[:, states:].T.astype(BF16)
    total_parts = split(jnp.broadcast_to(jnp.exp(last), (heads, LANES)).T[0:8, :], 3)

    arrivals[3].wait()

    def prepare(k, carry):
        at = pl.multiple_of(k * 2 * LANES, 2 * LANES)
        hot = one_hot(heads, 2 * LANES, at, head_size)
        spread = product(factor_parts[0], hot) + product(factor_parts[1], hot)
        weighted = (cotv[:, pl.ds(at, 2 * LANES)].astype(F32) * spread).astype(BF16)
        wc[:, pl.ds(at, 2 * LANES)] = weighted
        local = product(reads_t, weighted).astype(BF16)
        fl[2 * k] = local[:, :LANES]
        fl[2 * k + 1] = local[:, LANES:]
        return carry

    lax.fori_loop(0, tiles // 2, prepare, 0)
    for i in range(tiles):
        hot = one_hot(heads, LANES, i * LANES, head_size)
        spread = functools.reduce(jnp.add, [product(p, hot) for p in reversed(total_parts)])
        tot_s[i // group, i % group : i % group + 1, :] = spread[0:1, :]

    pl.semaphore_wait(barrier, nx - 1 + ny - 1)

    def tot_x_copy(d):
        to = lax.rem(x + d, nx)
        return send(tot_s.at[to], tot_x.at[x], tot_ss.at[d], tot_rs.at[d], {"seq_1": to})

    def x1_copy(g, d):
        to = lax.rem(x + d, nx)
        return send(fl.at[to * group + g], rx1.at[g, x], x1_ss.at[g, d], x1_rs.at[g, d], {"seq_1": to})

    def tot_y_copy(d):
        to = lax.rem(y + d, ny)
        return send(tots_y, tot_y.at[y], toty_ss.at[d], toty_rs.at[d], {"seq_0": to})

    def y1_copy(g, d):
        to = lax.rem(y + d, ny)
        part = pl.ds(pl.multiple_of(to * rows, rows), rows)
        return send(rs.at[g, part], ry1.at[g, y], y1_ss.at[g, d], y1_rs.at[g, d], {"seq_0": to})

    def y2_copy(g, d):
        to = lax.rem(y + d, ny)
        part = pl.ds(pl.multiple_of(y * rows, rows), rows)
        return send(bs.at[g, to], ry2.at[g, part], y2_ss.at[g, d], y2_rs.at[g, d], {"seq_0": to})

    def x2_copy(g, d):
        to = lax.rem(x + d, nx)
        return send(bx.at[g, to], by.at[x * group + g], x2_ss.at[g, d], x2_rs.at[g, d], {"seq_1": to})

    for d in range(1, nx):
        tot_x_copy(d).start()

    def start_x1(g, carry):
        for d in range(1, nx):
            x1_copy(g, d).start()
        rx1[g, x] = fl[x * group + g]
        return carry

    lax.fori_loop(0, group, start_x1, 0)
    tot_x[x] = tot_s[x]

    arrivals[4].wait()
    mm[...] = jnp.zeros_like(mm)
    far = jnp.where(
        lax.broadcasted_iota(jnp.int32, (LANES, LANES), 0)
        >= lax.broadcasted_iota(jnp.int32, (LANES, LANES), 1),
        0.0,
        FAR,
    )
    half = tokens // 2
    first_head = lax.broadcasted_iota(jnp.int32, (tokens, LANES), 1) < head_size

    def mix(i, carry):
        at = pl.multiple_of(i * LANES, LANES)
        ins = inv[:, pl.ds(at, LANES)]
        cots = cotv[:, pl.ds(at, LANES)]
        columns = cs_ref[...]
        cs_ref[...] = pltpu.roll(columns, LANES - 2, 1)
        for j in range(2):
            keep = first_head if j == 0 else jnp.logical_not(first_head)
            own = jnp.where(keep, ins, jnp.zeros_like(ins))
            scores = product_nt(cots, own)
            at_row = cum_ref[pl.ds(2 * i + j, 1), :]
            step_row = stepv[pl.ds(2 * i + j, 1), :]
            column = columns[:, j : j + 1]
            for a, b in ((0, 0), (1, 0), (1, 1)):
                ra = slice(a * half, (a + 1) * half)
                rb = slice(b * half, (b + 1) * half)
                gap = column[ra] - at_row[:, rb]
                if a == b:
                    gap = gap + far
                mm[ra, rb] += scores[ra, rb] * (jnp.exp(gap) * step_row[:, rb])
        return carry

    pairs = heads // 2
    lax.fori_loop(0, pairs // 2, mix, 0)

    for d in range(1, nx):
        tot_x_copy(d).wait_recv()
    total_y = tot_x[0]
    for k in range(1, nx):
        total_y = total_y * tot_x[k]
    tots_y[...] = total_y
    tot_y[y] = total_y
    for d in range(1, ny):
        tot_y_copy(d).start()

    def row_part(g, carry):
        for d in range(1, nx):
            x1_copy(g, d).wait_recv()
        state = rx1[g, nx - 1].astype(F32)
        for k in reversed(range(nx - 1)):
            state = rx1[g, k].astype(F32) + tot_x[k, pl.ds(g, 1), :] * state
        rs[g] = state.astype(BF16)
        ry1[g, y] = rs[g, pl.ds(pl.multiple_of(y * rows, rows), rows)]
        for d in range(1, ny):
            y1_copy(g, d).start()
        return carry

    lax.fori_loop(0, group, row_part, 0)

    lax.fori_loop(pairs // 2, pairs, mix, 0)

    for d in range(1, ny):
        tot_y_copy(d).wait_recv()

    def suffix(g, carry):
        for d in range(1, ny):
            y1_copy(g, d).wait_recv()
        state = jnp.zeros((rows, LANES), F32)
        for k in reversed(range(ny)):
            bs[g, k] = state.astype(BF16)
            if k:
                state = ry1[g, k].astype(F32) + tot_y[k, pl.ds(g, 1), :] * state
        ry2[g, pl.ds(pl.multiple_of(y * rows, rows), rows)] = bs[g, y]
        for d in range(1, ny):
            y2_copy(g, d).start()
        return carry

    lax.fori_loop(0, group, suffix, 0)

    entering = ei_ref[...].T
    entering_parts = split(entering, 2)

    def weigh(k, carry):
        at = pl.multiple_of(k * 2 * LANES, 2 * LANES)
        hot = one_hot(heads, 2 * LANES, at, head_size)
        spread = product(entering_parts[0], hot) + product(entering_parts[1], hot)
        wi[:, pl.ds(at, 2 * LANES)] = (inv[:, pl.ds(at, 2 * LANES)].astype(F32) * spread).astype(BF16)
        return carry

    lax.fori_loop(0, tiles // 2, weigh, 0)

    def expand(g, carry):
        for d in range(1, ny):
            y2_copy(g, d).wait_recv()
        state = ry2[g].astype(F32)
        for k in reversed(range(nx)):
            bx[g, k] = state.astype(BF16)
            if k:
                state = rx1[g, k].astype(F32) + tot_x[k, pl.ds(g, 1), :] * state
        by[x * group + g] = bx[g, x]
        for d in range(1, nx):
            x2_copy(g, d).start()
        return carry

    lax.fori_loop(0, group, expand, 0)

    arrivals[5].wait()
    arrivals[6].wait()
    mixing = mm[...]
    reads = act_ref[:, states:]
    writes = act_ref[:, :states]
    inner_write = product(mixing.T.astype(BF16), reads)
    inner_read = product(mixing.astype(BF16), writes)
    grad_read = inner_read + product(wc[...], esv[...])
    read_side = (grad_read * slope_ref[:, states:]).astype(BF16)
    sig_ref[:, states:] = read_side
    eye = jnp.where(
        lax.broadcasted_iota(jnp.int32, (LANES, LANES), 0)
        == lax.broadcasted_iota(jnp.int32, (LANES, LANES), 1),
        1.0,
        0.0,
    ).astype(BF16)

    def turn(k, carry):
        at = pl.multiple_of(k * LANES, LANES)
        piece = xv[:, pl.ds(at, LANES)]
        pk_ref[pl.ds(k, 1), :] = jnp.max(jnp.abs(piece.astype(F32)), axis=0, keepdims=True)
        turned = product_nt(eye, piece).astype(BF16)
        xt[pl.ds(at, LANES), :] = turned
        g_ref[1, pl.ds(at, LANES), :] = product(turned, read_side).astype(BF16)
        return carry

    lax.fori_loop(0, width // LANES, turn, 0)

    def wait_x2(g, carry):
        for d in range(1, nx):
            x2_copy(g, d).wait_recv()
        return carry

    lax.fori_loop(0, group, wait_x2, 0)
    carried = product_nt(wi[:, 0:LANES], by[0])
    for i in range(1, tiles):
        carried = carried + product_nt(wi[:, i * LANES : (i + 1) * LANES], by[i])
    write_side = ((inner_write + carried) * slope_ref[:, :states]).astype(BF16)
    sig_ref[:, :states] = write_side

    def finish(k, carry):
        at = pl.multiple_of(k * 2 * LANES, 2 * LANES)
        g_ref[0, pl.ds(at, 2 * LANES), :] = product(xt[pl.ds(at, 2 * LANES), :], write_side).astype(BF16)
        return carry

    lax.fori_loop(0, width // (2 * LANES), finish, 0)

    for d in range(1, nx):
        tot_x_copy(d).wait_send()
    for d in range(1, ny):
        tot_y_copy(d).wait_send()

    def drain(g, carry):
        for d in range(1, nx):
            x1_copy(g, d).wait_send()
            x2_copy(g, d).wait_send()
        for d in range(1, ny):
            y1_copy(g, d).wait_send()
            y2_copy(g, d).wait_send()
        return carry

    lax.fori_loop(0, group, drain, 0)


def reduce_kernel(
    sizes,
    g_ref, pk_in,
    out_ref, pk_out,
    pair, sx, rx, s2, ry, acc, s4, r4, pk_a, pk_b, pk_x, pk_y, pk_z,
    pair_ss, pair_rs, x_ss, x_rs, y_ss, y_rs, z_ss, z_rs,
    pkx_ss, pkx_rs, pky_ss, pky_rs, pkz_ss, pkz_rs,
):
    ny, nx, nz, nc = sizes
    width, states = g_ref.shape[1:]
    block = width // ny
    part = block // nx
    final = part // (nz * nc)
    y = lax.axis_index("seq_0")
    x = lax.axis_index("seq_1")
    z = lax.axis_index("dp_0")
    c = lax.axis_index("dp_1")
    other = 1 - c
    mine = z * nc + c
    ends = nz * nc

    def place(d):
        to = lax.rem(mine + d, ends)
        return to, {"dp_0": to // nc, "dp_1": lax.rem(to, nc)}

    barrier = pltpu.get_barrier_semaphore()
    for d in range(1, nx):
        pl.semaphore_signal(barrier, inc=1, device_id={"seq_1": lax.rem(x + d, nx)}, device_id_type=MESH_ID)
    for d in range(1, ny):
        pl.semaphore_signal(barrier, inc=1, device_id={"seq_0": lax.rem(y + d, ny)}, device_id_type=MESH_ID)
    for d in range(1, ends):
        pl.semaphore_signal(barrier, inc=1, device_id=place(d)[1], device_id_type=MESH_ID)
    pl.semaphore_wait(barrier, nx - 1 + ny - 1 + ends - 1)

    def block_at(k):
        return lax.rem(y + 1 + k, ny)

    def pair_copy(k):
        at = pl.ds(pl.multiple_of(block_at(k) * block, block), block)
        return send(g_ref.at[other, at], pair.at[at], pair_ss.at[k], pair_rs.at[k], {"dp_1": other})

    def x_copy(k, d):
        to = lax.rem(x + d, nx)
        return send(sx.at[k, to], rx.at[k, d], x_ss.at[k, d], x_rs.at[k, d], {"seq_1": to})

    def y_copy(k):
        to = block_at(k)
        return send(s2.at[k], ry.at[k], y_ss.at[k], y_rs.at[k], {"seq_0": to})

    def z_copy(d):
        to, where = place(d)
        return send(s4.at[to], r4.at[mine], z_ss.at[d], z_rs.at[d], where)

    def pkx_copy(d):
        return send(pk_in, pk_x.at[d], pkx_ss.at[d], pkx_rs.at[d], {"seq_1": lax.rem(x + d, nx)})

    def pky_copy(d):
        return send(pk_a, pk_y.at[d], pky_ss.at[d], pky_rs.at[d], {"seq_0": lax.rem(y + d, ny)})

    def pkz_copy(d):
        return send(pk_b, pk_z.at[d], pkz_ss.at[d], pkz_rs.at[d], place(d)[1])

    for k in range(ny):
        pair_copy(k).start()
    for d in range(1, nx):
        pkx_copy(d).start()

    def first(k, carry):
        pair_copy(k).wait_recv()
        base = pl.multiple_of(block_at(k) * block, block)
        for j in range(nx):
            at = pl.ds(pl.multiple_of(base + j * part, part), part)
            total = g_ref[c, at].astype(F32) + pair[at].astype(F32)
            sx[k, j] = total.astype(BF16)
        for d in range(1, nx):
            x_copy(k, d).start()
        return carry

    lax.fori_loop(0, ny, first, 0)

    for d in range(1, nx):
        pkx_copy(d).wait_recv()
    top = pk_in[...]
    for d in range(1, nx):
        top = jnp.maximum(top, pk_x[d])
    pk_a[...] = top
    for d in range(1, ny):
        pky_copy(d).start()

    def second(k, carry):
        base = pl.multiple_of(block_at(k) * block + x * part, part)
        at = pl.ds(base, part)
        total = g_ref[c, at].astype(F32) + pair[at].astype(F32)
        for d in range(1, nx):
            x_copy(k, d).wait_recv()
            total = total + rx[k, d].astype(F32)

        @pl.when(k < ny - 1)
        def _():
            s2[k] = total.astype(BF16)
            y_copy(k).start()

        acc[...] = total
        return carry

    lax.fori_loop(0, ny, second, 0)

    for d in range(1, ny):
        pky_copy(d).wait_recv()
    top = pk_a[...]
    for d in range(1, ny):
        top = jnp.maximum(top, pk_y[d])
    pk_b[...] = top
    for d in range(1, ends):
        pkz_copy(d).start()

    total = acc[...]
    for k in range(ny - 1):
        y_copy(k).wait_recv()
        total = total + ry[k].astype(F32)
    s4[...] = jnp.zeros_like(s4)
    for q in range(ends):
        s4[q, 0:final, :] = total[q * final : (q + 1) * final, :]
    r4[mine] = s4[mine]
    for d in range(1, ends):
        z_copy(d).start()
    for d in range(1, ends):
        pkz_copy(d).wait_recv()
    top = pk_b[...]
    for d in range(1, ends):
        top = jnp.maximum(top, pk_z[d])
    pk_out[...] = top
    for d in range(1, ends):
        z_copy(d).wait_recv()
    for h in range(nc):
        total = r4[h]
        for k in range(1, nz):
            total = total + r4[k * nc + h]
        out_ref[:, h * states : (h + 1) * states] = total

    for k in range(ny):
        pair_copy(k).wait_send()
        for d in range(1, nx):
            x_copy(k, d).wait_send()
    for k in range(ny - 1):
        y_copy(k).wait_send()
    for d in range(1, nx):
        pkx_copy(d).wait_send()
    for d in range(1, ny):
        pky_copy(d).wait_send()
    for d in range(1, ends):
        pkz_copy(d).wait_send()
        z_copy(d).wait_send()


def on_device(
    sizes, layer_input, scan_input, scan_cotangent, step_size, log_decay, state_inputs, entry_state
):
    ny, nx, nz, nc = sizes
    tokens, width = layer_input.shape[1:]
    channels = scan_input.shape[2]
    heads = step_size.shape[1]
    states = state_inputs.shape[2] // 2
    tiles = channels // LANES
    group = tiles // nx
    padded = -(-group // 8) * 8
    rows = states // ny
    wide = width // LANES
    wide_pad = -(-wide // 8) * 8
    dma = pltpu.SemaphoreType.DMA
    vmem = pl.BlockSpec(memory_space=pltpu.VMEM)
    anywhere = pl.BlockSpec(memory_space=pl.ANY)
    big = (tokens, channels)
    state = (LANES, LANES)
    assert states == LANES and tokens == 2 * LANES
    sig, partial, local_peaks = pl.pallas_call(
        functools.partial(scan_kernel, (ny, nx)),
        out_shape=(
            jax.ShapeDtypeStruct((tokens, 2 * states), BF16),
            jax.ShapeDtypeStruct((2, width, states), BF16),
            jax.ShapeDtypeStruct((wide_pad, LANES), F32),
        ),
        in_specs=[anywhere] * 7,
        out_specs=(vmem, vmem, vmem),
        scratch_shapes=[
            pltpu.VMEM((tokens, width), BF16),
            pltpu.VMEM(big, BF16),
            pltpu.VMEM(big, BF16),
            pltpu.VMEM((heads, tokens), F32),
            pltpu.VMEM((heads, tokens), F32),
            pltpu.VMEM((tokens, 2 * states), BF16),
            pltpu.VMEM((channels, states), BF16),
            pltpu.VMEM(big, BF16),
            pltpu.VMEM(big, BF16),
            pltpu.VMEM((width, tokens), BF16),
            pltpu.VMEM((tiles, *state), BF16),
            pltpu.VMEM((tiles, *state), BF16),
            pltpu.VMEM((group, nx, *state), BF16),
            pltpu.VMEM((nx, padded, LANES), F32),
            pltpu.VMEM((nx, padded, LANES), F32),
            pltpu.VMEM((padded, LANES), F32),
            pltpu.VMEM((ny, padded, LANES), F32),
            pltpu.VMEM((group, *state), BF16),
            pltpu.VMEM((group, ny, rows, LANES), BF16),
            pltpu.VMEM((group, ny, rows, LANES), BF16),
            pltpu.VMEM((group, *state), BF16),
            pltpu.VMEM((group, nx, *state), BF16),
            pltpu.VMEM((tokens, tokens), F32),
            pltpu.VMEM((heads, tokens), F32),
            pltpu.VMEM((tokens, LANES), F32),
            pltpu.VMEM((heads, tokens), F32),
            pltpu.VMEM((tokens, 2 * states), F32),
            pltpu.VMEM((tokens, 2 * states), BF16),
            dma((7,)),
            dma((nx,)), dma((nx,)),
            dma((group, nx)), dma((group, nx)),
            dma((ny,)), dma((ny,)),
            dma((group, ny)), dma((group, ny)),
            dma((group, ny)), dma((group, ny)),
            dma((group, nx)), dma((group, nx)),
        ],
        compiler_params=pltpu.CompilerParams(
            collective_id=0, has_side_effects=True, vmem_limit_bytes=VMEM_BYTES
        ),
        name="scan",
    )(
        layer_input.reshape(tokens, width),
        scan_input.reshape(tokens, channels),
        scan_cotangent.reshape(tokens, channels),
        step_size.reshape(heads, tokens),
        log_decay.reshape(heads, tokens),
        state_inputs.reshape(tokens, 2 * states),
        entry_state.reshape(channels, states),
    )
    block = width // ny
    part = block // nx
    ends = nz * nc
    final = part // ends
    final_pad = -(-final // 8) * 8
    peak_tile = (wide_pad, LANES)
    summed, peaks = pl.pallas_call(
        functools.partial(reduce_kernel, sizes),
        out_shape=(
            jax.ShapeDtypeStruct((final_pad, 2 * states), F32),
            jax.ShapeDtypeStruct(peak_tile, F32),
        ),
        in_specs=[vmem, vmem],
        out_specs=(vmem, vmem),
        scratch_shapes=[
            pltpu.VMEM((width, states), BF16),
            pltpu.VMEM((ny, nx, part, states), BF16),
            pltpu.VMEM((ny, nx, part, states), BF16),
            pltpu.VMEM((ny, part, states), BF16),
            pltpu.VMEM((ny, part, states), BF16),
            pltpu.VMEM((part, states), F32),
            pltpu.VMEM((ends, final_pad, states), F32),
            pltpu.VMEM((ends, final_pad, states), F32),
            pltpu.VMEM(peak_tile, F32),
            pltpu.VMEM(peak_tile, F32),
            pltpu.VMEM((nx, *peak_tile), F32),
            pltpu.VMEM((ny, *peak_tile), F32),
            pltpu.VMEM((ends, *peak_tile), F32),
            dma((ny,)), dma((ny,)),
            dma((ny, nx)), dma((ny, nx)),
            dma((ny,)), dma((ny,)),
            dma((ends,)), dma((ends,)),
            dma((nx,)), dma((nx,)),
            dma((ny,)), dma((ny,)),
            dma((ends,)), dma((ends,)),
        ],
        compiler_params=pltpu.CompilerParams(
            collective_id=1, has_side_effects=True, vmem_limit_bytes=VMEM_BYTES
        ),
        name="reduce",
    )(partial, local_peaks)
    where = ((lax.axis_index("seq_0") * nx + lax.axis_index("seq_1")) * nz + lax.axis_index("dp_0")) * nc
    where = (where + lax.axis_index("dp_1")) * final
    own_peaks = lax.dynamic_slice(peaks[:wide].reshape(width), (where,), (final,))
    grad = summed[:final] * (1.0 / (own_peaks + EPSILON))[:, None]
    return (sig.reshape(1, tokens, 2 * states), grad)


def arranged(devices, sizes):
    torus = Mesh(devices.reshape(sizes), AXES)
    placed = (
        P(DP, SEQ, None),
        P(DP, SEQ, None),
        P(DP, SEQ, None),
        P(DP, None, SEQ),
        P(DP, None, SEQ),
        P(DP, SEQ, None),
        P(DP, SEQ, None, None),
    )
    return jax.shard_map(
        functools.partial(on_device, sizes),
        mesh=torus,
        in_specs=placed,
        out_specs=(P(DP, SEQ, None), P(AXES, None)),
        check_vma=False,
    )


def solution(mesh):
    return arranged(mesh.devices, (8, 4, 8, 2))
```

time: 215 us -> 80.3 us (0.37)
  blocking collectives: 113 us -> 0 us
  Pallas kernels: 0 us -> 76.5 us
  waiting for transfers between devices: 41.2 us -> 0 us
  other arithmetic: 18.6 us -> 1.45 us
  between operations: 15 us -> 0.67 us
  matrix products: 10.2 us -> 0 us
  local copies, waits for them, and re-layouts: 9.6 us -> 1.37 us
  starting transfers between devices: 6.31 us -> 0 us
    pallas_call x0 -> x2, Pallas kernels: none -> 76.5 us  [the longest x1 41.7 us: on_device(): pl.pallas_call(functools.partial(scan_kernel, (ny, nx)), out_shape=(jax.S...]
    pmax x4 -> x0, blocking collectives: 51.5 us -> none  [by_axis(): return functools.reduce(lax.pmax, axes, x)]
    all_to_all x1 -> x0, blocking collectives: 39.4 us -> none  [sent_and_summed(): lax.all_to_all(tiles, axis, split_axis=0, concat_axis=0, tiled=True)]
    all_gather x2 -> x0, waiting for transfers between devices: 33 us -> none  [prefix_by_axis(): lax.all_gather(part.astype(kind), axis)]
    convert_element_type x10 -> x0, other arithmetic: 14.2 us -> none  [the longest x1 6.07 us: on_device(): state_now.astype(jnp.bfloat16).reshape(seq_local, channels, states)]
    all_gather x1 -> x0, blocking collectives: 13.3 us -> none  [prefix_by_axis(): lax.all_gather(part.astype(kind), axis)]
    dot_general x7 -> x0, matrix products: 10.2 us -> none  [the longest x1 5.74 us: block_inner(): jnp.einsum('shp,thp->hst', cotangents, inputs, preferred_element_type=jnp...]
    unnamed x1 -> x0, blocking collectives: 9.26 us -> none
  transfers between devices with their start and end apart: 3 -> 0, of which waited for: 2 -> 0; matrix products, arithmetic and copies ran while one was open for 9% -> 0% of each run, Pallas kernels for 0% -> 0%
where the time goes in v1:
time: 80.3 us; the launch traced here: 80 us
  Pallas kernels  76.5 us (95%)
  other arithmetic  1.45 us (2%)
  local copies, waits for them, and re-layouts  1.37 us (2%)
    pallas_call x1, Pallas kernels, on_device(): pl.pallas_call(functools.partial(scan_kernel, (ny, nx)), out_shape=(jax.S...  41.7 us
    pallas_call x1, Pallas kernels, on_device(): pl.pallas_call(functools.partial(reduce_kernel, sizes), out_shape=(jax.Sh...  34.8 us

profile of v1, /device:TPU:1, one launch (start us, length us, event | category | flops | bytes accessed | tf_op | source)
XLA Modules:
  0.0 80.0 jit_solution(17111306963867718650)
XLA Ops:
  0.6 41.7 %scan.1 = (bf16[256,256]{1,0:T(8,128)(2,1)}, bf16[2,2560,128]{2,1,0:T(8,128)(2,1)}, f32[24,128]{1,0:T(8,128)}) custom-call(bf16[256,2560]{1,0:T(8,128)(2,1)} %bitcast.10, bf16[256,2560]{1,0:T(8,128)(2,1)} %bitcast.11, bf16[256,2560]{1,0:T(8,128)(2,1)} %bitcast.12, f32[40,256]{1,0:T(8,128)} %bitcast.16, f32[40,256]{1,0:T(8,128)} %bitcast.17, ...), custom_call_target="tpu_custom_call" | custom-call | tf_op jit(solution)/shard_map/scan/pallas_call | solution.py:524
  42.4 0.0 copy-start
  42.4 34.8 %reduce.1 = (f32[8,256]{1,0:T(8,128)}, f32[24,128]{1,0:T(8,128)}) custom-call(bf16[2,2560,128]{2,1,0:T(8,128)(2,1)} %get-tuple-element.8.g_ref, f32[24,128]{1,0:T(8,128)} %get-tuple-element.9.pk_in), custom_call_target="tpu_custom_call" | custom-call | tf_op jit(solution)/shard_map/reduce/pallas_call | solution.py:589
  77.2 0.7 slice_bitcast_fusion
  77.9 0.1 add_divide_fusion
  78.0 1.4 %slice_multiply_fusion = f32[5,256]{1,0:T(8,128)} fusion(f32[8,256]{1,0:T(8,128)} %get-tuple-element.10, f32[5]{0:T(128)S(1)} %add_divide_fusion), kind=kLoop, calls=%fused_computation.1 | loop fusion | flops 1280 | bytes 10260 | tf_op jit(solution)/shard_map/mul | solution.py:627
  79.3 0.0 copy-done
  79.3 0.7 copy.10
Async XLA Ops:
  42.4 37.0 %copy-start = (bf16[256,256]{1,0:T(8,128)(2,1)S(1)}, bf16[256,256]{1,0:T(8,128)(2,1)}, u32[]{:S(2)}) copy-start(bf16[256,256]{1,0:T(8,128)(2,1)} %get-tuple-element.7) | copy-start | bytes 393220

commit v2 on v1

v2 whole, which is shorter than its diff:
```python
import functools

import jax
import jax.numpy as jnp
from jax import lax
from jax.experimental import pallas as pl
from jax.experimental.pallas import tpu as pltpu
from jax.sharding import Mesh
from jax.sharding import PartitionSpec as P

AXES = ("seq_0", "seq_1", "dp_0", "dp_1")
SEQ = ("seq_0", "seq_1")
DP = ("dp_0", "dp_1")
MESH_ID = pl.DeviceIdType.MESH
F32 = jnp.float32
BF16 = jnp.bfloat16
EPSILON = 1e-06
LANES = 128
FAR = -1.0e9
VMEM_BYTES = 60 * 1024 * 1024


def product(a, b):
    return lax.dot_general(a, b, (((1,), (0,)), ((), ())), preferred_element_type=F32)


def product_nt(a, b):
    return lax.dot_general(a, b, (((1,), (1,)), ((), ())), preferred_element_type=F32)


def split(x, parts):
    pieces = []
    for _ in range(parts):
        piece = x.astype(BF16)
        pieces.append(piece)
        x = x - piece.astype(F32)
    return pieces


def one_hot(heads, width, first, head_size):
    row = lax.broadcasted_iota(jnp.int32, (heads, width), 0)
    lane = lax.broadcasted_iota(jnp.int32, (heads, width), 1) + first
    start = row * head_size
    return jnp.where((lane >= start) & (lane < start + head_size), 1.0, 0.0).astype(BF16)


def send(src, dst, send_sem, recv_sem, where):
    return pltpu.make_async_remote_copy(
        src_ref=src,
        dst_ref=dst,
        send_sem=send_sem,
        recv_sem=recv_sem,
        device_id=where,
        device_id_type=MESH_ID,
    )


def scan_kernel(
    sizes,
    x_hbm, in_hbm, cot_hbm, step_hbm, ld_hbm, si_hbm, es_hbm,
    sig_ref, out_ref,
    xv, inv, cotv, stepv, ldv, siv, esv,
    wc, wi, xt, fl, by, rx1, tot_s, tot_x, tots_y, tot_y, rs, ry1, bs, ry2, bx,
    mm, cum_ref, cs_ref, ei_ref, slope_ref, act_ref,
    gr, gw, pair_r, pair_w, sy, ry, sxr, rxr, sx, rx, s2, r2, sz, rz, px_s, px_r, py_s, py_r, pz_s, pz_r,
    in_sem, tot_ss, tot_rs, x1_ss, x1_rs, toty_ss, toty_rs, y1_ss, y1_rs, y2_ss, y2_rs, x2_ss, x2_rs,
    pr_ss, pr_rs, pw_ss, pw_rs, gy_ss, gy_rs, gx_ss, gx_rs, wx_ss, wx_rs, wy_ss, wy_rs, z_ss, z_rs,
    px_ss, px_rs, py_ss, py_rs, pz_ss, pz_rs,
):
    ny, nx, nz, nc = sizes
    tokens, width = xv.shape
    channels = inv.shape[1]
    heads = ldv.shape[0]
    head_size = channels // heads
    states = act_ref.shape[1] // 2
    tiles = channels // LANES
    group = tiles // nx
    rows = states // ny
    part = width // (ny * nx)
    half = part // nc
    ends = nz * nc
    final = part // ends
    share = ends // nc
    y = lax.axis_index("seq_0")
    x = lax.axis_index("seq_1")
    z = lax.axis_index("dp_0")
    c = lax.axis_index("dp_1")
    other = 1 - c
    mine = z * nc + c

    def beside(d):
        return lax.rem(x + d, nx)

    def along(d):
        return lax.rem(y + d, ny)

    def place(to):
        return {"dp_0": to // nc, "dp_1": lax.rem(to, nc)}

    arrivals = [
        pltpu.make_async_copy(src, dst, in_sem.at[i])
        for i, (src, dst) in enumerate(
            (
                (ld_hbm, ldv), (si_hbm, siv), (cot_hbm, cotv), (step_hbm, stepv),
                (in_hbm, inv), (es_hbm, esv), (x_hbm, xv),
            )
        )
    ]
    for copy in arrivals:
        copy.start()

    barrier = pltpu.get_barrier_semaphore()
    for d in range(1, nx):
        pl.semaphore_signal(barrier, inc=1, device_id={"seq_1": beside(d)}, device_id_type=MESH_ID)
    for d in range(1, ny):
        pl.semaphore_signal(barrier, inc=1, device_id={"seq_0": along(d)}, device_id_type=MESH_ID)
    for d in range(1, ends):
        pl.semaphore_signal(
            barrier, inc=1, device_id=place(lax.rem(mine + d, ends)), device_id_type=MESH_ID
        )

    arrivals[0].wait()
    upper = (
        lax.broadcasted_iota(jnp.int32, (tokens, tokens), 0)
        <= lax.broadcasted_iota(jnp.int32, (tokens, tokens), 1)
    )
    ones = jnp.where(upper, 1.0, 0.0).astype(BF16)
    cum = functools.reduce(jnp.add, [product(p, ones) for p in reversed(split(ldv[...], 3))])
    last = cum[:, tokens - 1 : tokens]
    cum_ref[...] = cum
    cs_ref[:, 0:heads] = cum.T
    factor_parts = split(jnp.exp(cum).T, 2)
    total_parts = split(jnp.broadcast_to(jnp.exp(last), (heads, LANES)).T[0:8, :], 3)
    arrivals[1].wait()
    preact = siv[...].astype(F32)
    sigma = 1.0 / (1.0 + jnp.exp(-preact))
    act = preact * sigma
    slope_ref[...] = sigma * (1.0 + preact * (1.0 - sigma))
    act_ref[...] = act.astype(BF16)
    reads_t = act[:, states:].T.astype(BF16)

    arrivals[2].wait()
    for at in range(0, channels, 2 * LANES):
        hot = one_hot(heads, 2 * LANES, at, head_size)
        spread = product(factor_parts[0], hot) + product(factor_parts[1], hot)
        weighted = (cotv[:, at : at + 2 * LANES].astype(F32) * spread).astype(BF16)
        wc[:, at : at + 2 * LANES] = weighted
        local = product(reads_t, weighted).astype(BF16)
        fl[at // LANES] = local[:, :LANES]
        fl[at // LANES + 1] = local[:, LANES:]
    for i in range(tiles):
        hot = one_hot(heads, LANES, i * LANES, head_size)
        spread = functools.reduce(jnp.add, [product(p, hot) for p in reversed(total_parts)])
        tot_s[i // group, i % group : i % group + 1, :] = spread[0:1, :]

    pl.semaphore_wait(barrier, nx - 1 + ny - 1 + ends - 1)

    def tot_x_copy(d):
        to = beside(d)
        return send(tot_s.at[to], tot_x.at[x], tot_ss.at[d], tot_rs.at[d], {"seq_1": to})

    def x1_copy(g, d):
        to = beside(d)
        return send(fl.at[to * group + g], rx1.at[g, x], x1_ss.at[g, d], x1_rs.at[g, d], {"seq_1": to})

    def tot_y_copy(d):
        return send(tots_y, tot_y.at[y], toty_ss.at[d], toty_rs.at[d], {"seq_0": along(d)})

    def y1_copy(g, d):
        to = along(d)
        return send(
            rs.at[g, pl.ds(pl.multiple_of(to * rows, rows), rows)],
            ry1.at[g, y], y1_ss.at[g, d], y1_rs.at[g, d], {"seq_0": to},
        )

    def y2_copy(g, d):
        to = along(d)
        return send(
            bs.at[g, to],
            ry2.at[g, pl.ds(pl.multiple_of(y * rows, rows), rows)],
            y2_ss.at[g, d], y2_rs.at[g, d], {"seq_0": to},
        )

    def x2_copy(g, d):
        to = beside(d)
        return send(bx.at[g, to], by.at[x * group + g], x2_ss.at[g, d], x2_rs.at[g, d], {"seq_1": to})

    def pair_r_copy():
        return send(gr.at[:, :, other], pair_r, pr_ss, pr_rs, {"dp_1": other})

    def pair_w_copy(k):
        to = along(1 + k)
        return send(gw.at[to, :, other], pair_w.at[to], pw_ss.at[k], pw_rs.at[k], {"dp_1": other})

    def gy_copy(d):
        return send(sy.at[d], ry.at[d], gy_ss.at[d], gy_rs.at[d], {"seq_0": along(d)})

    def gx_copy(d):
        return send(sxr.at[beside(d)], rxr.at[d], gx_ss.at[d], gx_rs.at[d], {"seq_1": beside(d)})

    def wx_copy(k, d):
        return send(sx.at[k, d], rx.at[k, d], wx_ss.at[k, d], wx_rs.at[k, d], {"seq_1": beside(d)})

    def wy_copy(k):
        return send(s2.at[k], r2.at[k], wy_ss.at[k], wy_rs.at[k], {"seq_0": along(1 + k)})

    def px_copy(d):
        return send(px_s.at[beside(d)], px_r.at[d], px_ss.at[d], px_rs.at[d], {"seq_1": beside(d)})

    def py_copy(d):
        return send(py_s.at[along(d)], py_r.at[d], py_ss.at[d], py_rs.at[d], {"seq_0": along(d)})

    def pz_copy(d):
        to = lax.rem(mine + d, ends)
        return send(pz_s, pz_r.at[d], pz_ss.at[d], pz_rs.at[d], place(to))

    def z_copy(side, i):
        to = c * share + i
        return send(sz.at[side, i], rz.at[side, z], z_ss.at[side, i], z_rs.at[side, z], place(to))

    def z_arrival(side, k):
        return send(sz.at[side, 0], rz.at[side, k], z_ss.at[side, 0], z_rs.at[side, k], place(mine))

    def start_z(side, total):
        for i in range(share):
            sz[side, i, 0:final, :] = total[i * final : (i + 1) * final, :]
        for i in range(share):
            to = c * share + i

            @pl.when(to != mine)
            def _():
                z_copy(side, i).start()

            @pl.when(to == mine)
            def _():
                rz[side, z] = sz[side, i]

    for d in range(1, nx):
        tot_x_copy(d).start()
    for g in range(group):
        for d in range(1, nx):
            x1_copy(g, d).start()
    for g in range(group):
        rx1[g, x] = fl[x * group + g]
    tot_x[x] = tot_s[x]

    arrivals[3].wait()
    ei_ref[...] = stepv[...] * jnp.exp(last - cum_ref[...])
    arrivals[4].wait()
    mm[...] = jnp.zeros_like(mm)
    far = jnp.where(
        lax.broadcasted_iota(jnp.int32, (LANES, LANES), 0)
        >= lax.broadcasted_iota(jnp.int32, (LANES, LANES), 1),
        0.0,
        FAR,
    )
    middle = tokens // 2
    first_head = lax.broadcasted_iota(jnp.int32, (tokens, LANES), 1) < head_size

    def mix(i, carry):
        at = pl.multiple_of(i * LANES, LANES)
        ins = inv[:, pl.ds(at, LANES)]
        cots = cotv[:, pl.ds(at, LANES)]
        columns = cs_ref[...]
        cs_ref[...] = pltpu.roll(columns, LANES - 2, 1)
        sums = {}
        for j in range(2):
            keep = first_head if j == 0 else jnp.logical_not(first_head)
            own = jnp.where(keep, ins, jnp.zeros_like(ins))
            scores = product_nt(cots, own)
            at_row = cum_ref[pl.ds(2 * i + j, 1), :]
            step_row = stepv[pl.ds(2 * i + j, 1), :]
            column = columns[:, j : j + 1]
            for a, b in ((0, 0), (1, 0), (1, 1)):
                ra = slice(a * middle, (a + 1) * middle)
                rb = slice(b * middle, (b + 1) * middle)
                gap = column[ra] - at_row[:, rb]
                if a == b:
                    gap = gap + far
                term = scores[ra, rb] * (jnp.exp(gap) * step_row[:, rb])
                sums[a, b] = term if j == 0 else sums[a, b] + term
        for a, b in ((0, 0), (1, 0), (1, 1)):
            mm[a * middle : (a + 1) * middle, b * middle : (b + 1) * middle] += sums[a, b]
        return carry

    lax.fori_loop(0, heads // 2, mix, 0)

    for d in range(1, nx):
        tot_x_copy(d).wait_recv()
    total_y = tot_x[0]
    for k in range(1, nx):
        total_y = total_y * tot_x[k]
    tots_y[...] = total_y
    tot_y[y] = total_y
    for d in range(1, ny):
        tot_y_copy(d).start()

    def row_part(g):
        for d in range(1, nx):
            x1_copy(g, d).wait_recv()
        state = rx1[g, nx - 1].astype(F32)
        for k in reversed(range(nx - 1)):
            state = rx1[g, k].astype(F32) + tot_x[k, g : g + 1, :] * state
        rs[g] = state.astype(BF16)
        ry1[g, y] = rs[g, pl.ds(pl.multiple_of(y * rows, rows), rows)]
        for d in range(1, ny):
            y1_copy(g, d).start()

    def suffix(g):
        if g == 0:
            for d in range(1, ny):
                tot_y_copy(d).wait_recv()
        for d in range(1, ny):
            y1_copy(g, d).wait_recv()
        state = jnp.zeros((rows, LANES), F32)
        for k in reversed(range(ny)):
            bs[g, k] = state.astype(BF16)
            if k:
                state = ry1[g, k].astype(F32) + tot_y[k, g : g + 1, :] * state
        ry2[g, pl.ds(pl.multiple_of(y * rows, rows), rows)] = bs[g, y]
        for d in range(1, ny):
            y2_copy(g, d).start()

    def expand(g):
        for d in range(1, ny):
            y2_copy(g, d).wait_recv()
        state = ry2[g].astype(F32)
        for k in reversed(range(nx)):
            bx[g, k] = state.astype(BF16)
            if k:
                state = rx1[g, k].astype(F32) + tot_x[k, g : g + 1, :] * state
        by[x * group + g] = bx[g, x]
        for d in range(1, nx):
            x2_copy(g, d).start()

    row_part(0)
    arrivals[5].wait()
    mixing = mm[...]
    reads = act_ref[:, states:]
    writes = act_ref[:, :states]
    inner_read = product(mixing.astype(BF16), writes)
    grad_read = inner_read + product(wc[...], esv[...])
    read_side = (grad_read * slope_ref[:, states:]).astype(BF16)
    sig_ref[:, states:] = read_side
    row_part(1)
    arrivals[6].wait()
    eye = jnp.where(
        lax.broadcasted_iota(jnp.int32, (LANES, LANES), 0)
        == lax.broadcasted_iota(jnp.int32, (LANES, LANES), 1),
        1.0,
        0.0,
    ).astype(BF16)
    for at in range(0, width, LANES):
        xt[at : at + LANES, :] = product_nt(eye, xv[:, at : at + LANES]).astype(BF16)
    row_part(2)

    def gradient(side_value, store, b):
        block = nx * part
        value = product(xt[b * block : (b + 1) * block, :], side_value)
        for k in range(nx):
            for h in range(nc):
                at = k * part + h * half
                store[b, k, h] = value[at : at + half, :].astype(BF16)

    for b in range(ny):
        gradient(read_side, gr, b)
    pair_r_copy().start()
    row_part(3) if group > 3 else None
    suffix(0)
    for g in range(4, group):
        row_part(g)
    inner_write = product(mixing.T.astype(BF16), reads)
    suffix(1)

    entering_parts = split(ei_ref[...].T, 2)
    for at in range(0, channels, 2 * LANES):
        hot = one_hot(heads, 2 * LANES, at, head_size)
        spread = product(entering_parts[0], hot) + product(entering_parts[1], hot)
        wi[:, at : at + 2 * LANES] = (inv[:, at : at + 2 * LANES].astype(F32) * spread).astype(BF16)
    suffix(2)

    peaks = jnp.max(jnp.abs(xv[...].astype(F32)), axis=0, keepdims=True)
    padded = px_s.shape[2]
    owners = lax.broadcasted_iota(jnp.int32, (nx * ny, width), 0)
    start = sum(
        jnp.where((owners >= k * ny) & (owners < (k + 1) * ny), k * part + (owners - k * ny) * nx * part, 0)
        for k in range(nx)
    )
    lane = lax.broadcasted_iota(jnp.int32, (nx * ny, width), 1)
    spread_peaks = jnp.where((lane >= start) & (lane < start + part), peaks, 0.0).astype(BF16)
    column = lax.broadcasted_iota(jnp.int32, (width, padded), 0).astype(F32)
    place_in = column - part * jnp.floor((column + 0.5) * (1.0 / part))
    target = lax.broadcasted_iota(jnp.int32, (width, padded), 1).astype(F32)
    pick = jnp.where(place_in == target, 1.0, 0.0).astype(BF16)
    own_peaks = product(spread_peaks, pick)
    for k in range(nx):
        px_s[k] = own_peaks[k * ny : (k + 1) * ny, :]
    for d in range(1, nx):
        px_copy(d).start()

    for g in range(3, group):
        suffix(g)
    pair_r_copy().wait_recv()
    for d in range(1, ny):
        to = along(d)
        sy[d] = (gr[to, :, c].astype(F32) + pair_r[to].astype(F32)).astype(BF16)
        gy_copy(d).start()
    for d in range(1, nx):
        px_copy(d).wait_recv()
    top = px_s[x]
    for d in range(1, nx):
        top = jnp.maximum(top, px_r[d])
    for k in range(ny):
        py_s[k] = top[k : k + 1, :]
    for d in range(1, ny):
        py_copy(d).start()
    for g in range(group):
        expand(g)

    for d in range(1, ny):
        py_copy(d).wait_recv()
    top = py_s[y]
    for d in range(1, ny):
        top = jnp.maximum(top, py_r[d])
    pz_s[...] = top
    for d in range(1, ends):
        pz_copy(d).start()

    for g in range(2):
        for d in range(1, nx):
            x2_copy(g, d).wait_recv()
    carried = inner_write
    for g in range(2):
        for k in range(nx):
            i = k * group + g
            carried = carried + product_nt(wi[:, i * LANES : (i + 1) * LANES], by[i])

    read_sum = gr[y, :, c].astype(F32) + pair_r[y].astype(F32)
    for d in range(1, ny):
        gy_copy(d).wait_recv()
        read_sum = read_sum + ry[d].astype(F32)
    sxr[...] = read_sum
    for d in range(1, nx):
        gx_copy(d).start()

    for g in range(2, group):
        for d in range(1, nx):
            x2_copy(g, d).wait_recv()
        for k in range(nx):
            i = k * group + g
            carried = carried + product_nt(wi[:, i * LANES : (i + 1) * LANES], by[i])
    write_side = (carried * slope_ref[:, :states]).astype(BF16)
    sig_ref[:, :states] = write_side

    for b in range(ny):
        gradient(write_side, gw, b)
    for k in range(ny):
        pair_w_copy(k).start()

    for d in range(1, nx):
        gx_copy(d).wait_recv()
    read_sum = sxr[x]
    for d in range(1, nx):
        read_sum = read_sum + rxr[d]
    start_z(1, read_sum)

    def first(k, carry):
        pair_w_copy(k).wait_recv()
        to = along(1 + k)
        for d in range(1, nx):
            at = beside(d)
            sx[k, d] = (gw[to, at, c].astype(F32) + pair_w[to, at].astype(F32)).astype(BF16)
            wx_copy(k, d).start()
        return carry

    lax.fori_loop(0, ny, first, 0)

    def gathered(k):
        to = along(1 + k)
        total = gw[to, x, c].astype(F32) + pair_w[to, x].astype(F32)
        for d in range(1, nx):
            wx_copy(k, d).wait_recv()
            total = total + rx[k, d].astype(F32)
        return total

    def second(k, carry):
        s2[k] = gathered(k).astype(BF16)
        wy_copy(k).start()
        return carry

    lax.fori_loop(0, ny - 1, second, 0)
    total = gathered(ny - 1)
    for k in range(ny - 1):
        wy_copy(k).wait_recv()
        total = total + r2[k].astype(F32)
    start_z(0, total)

    for d in range(1, ends):
        pz_copy(d).wait_recv()
    top = pz_s[...]
    for d in range(1, ends):
        top = jnp.maximum(top, pz_r[d])
    lane = lax.broadcasted_iota(jnp.int32, (final, padded), 1)
    row = lax.broadcasted_iota(jnp.int32, (final, padded), 0)
    peak = jnp.sum(jnp.where(lane == row + mine * final, top, 0.0), axis=1, keepdims=True)
    scale = 1.0 / (peak + EPSILON)
    for side in (1, 0):
        for k in range(nz):

            @pl.when(jnp.logical_or(k != z, c != mine // share))
            def _():
                z_arrival(side, k).wait_recv()

        total = rz[side, 0, 0:final]
        for k in range(1, nz):
            total = total + rz[side, k, 0:final]
        out_ref[:, side * states : (side + 1) * states] = total * scale

    for d in range(1, nx):
        tot_x_copy(d).wait_send()
        px_copy(d).wait_send()
        gx_copy(d).wait_send()
    for d in range(1, ny):
        tot_y_copy(d).wait_send()
        py_copy(d).wait_send()
        gy_copy(d).wait_send()
    for d in range(1, ends):
        pz_copy(d).wait_send()
    pair_r_copy().wait_send()

    def drain(g, carry):
        for d in range(1, nx):
            x1_copy(g, d).wait_send()
            x2_copy(g, d).wait_send()
        for d in range(1, ny):
            y1_copy(g, d).wait_send()
            y2_copy(g, d).wait_send()
        return carry

    lax.fori_loop(0, group, drain, 0)

    def drain_write(k, carry):
        pair_w_copy(k).wait_send()
        for d in range(1, nx):
            wx_copy(k, d).wait_send()
        return carry

    lax.fori_loop(0, ny, drain_write, 0)
    for k in range(ny - 1):
        wy_copy(k).wait_send()
    for side in range(2):
        for i in range(share):

            @pl.when(c * share + i != mine)
            def _():
                z_copy(side, i).wait_send()


def on_device(
    sizes, layer_input, scan_input, scan_cotangent, step_size, log_decay, state_inputs, entry_state
):
    ny, nx, nz, nc = sizes
    tokens, width = layer_input.shape[1:]
    channels = scan_input.shape[2]
    heads = step_size.shape[1]
    states = state_inputs.shape[2] // 2
    tiles = channels // LANES
    group = tiles // nx
    padded = -(-group // 8) * 8
    rows = states // ny
    part = width // (ny * nx)
    half = part // nc
    ends = nz * nc
    final = part // ends
    share = ends // nc
    final_pad = -(-final // 8) * 8
    peak_pad = -(-part // LANES) * LANES
    dma = pltpu.SemaphoreType.DMA
    vmem = pl.BlockSpec(memory_space=pltpu.VMEM)
    anywhere = pl.BlockSpec(memory_space=pl.ANY)
    big = (tokens, channels)
    state = (LANES, LANES)
    assert states == LANES and tokens == 2 * LANES and nc == 2
    sig, grad = pl.pallas_call(
        functools.partial(scan_kernel, sizes),
        out_shape=(
            jax.ShapeDtypeStruct((tokens, 2 * states), BF16),
            jax.ShapeDtypeStruct((final, 2 * states), F32),
        ),
        in_specs=[anywhere] * 7,
        out_specs=(vmem, vmem),
        scratch_shapes=[
            pltpu.VMEM((tokens, width), BF16),
            pltpu.VMEM(big, BF16),
            pltpu.VMEM(big, BF16),
            pltpu.VMEM((heads, tokens), F32),
            pltpu.VMEM((heads, tokens), F32),
            pltpu.VMEM((tokens, 2 * states), BF16),
            pltpu.VMEM((channels, states), BF16),
            pltpu.VMEM(big, BF16),
            pltpu.VMEM(big, BF16),
            pltpu.VMEM((width, tokens), BF16),
            pltpu.VMEM((tiles, *state), BF16),
            pltpu.VMEM((tiles, *state), BF16),
            pltpu.VMEM((group, nx, *state), BF16),
            pltpu.VMEM((nx, padded, LANES), F32),
            pltpu.VMEM((nx, padded, LANES), F32),
            pltpu.VMEM((padded, LANES), F32),
            pltpu.VMEM((ny, padded, LANES), F32),
            pltpu.VMEM((group, *state), BF16),
            pltpu.VMEM((group, ny, rows, LANES), BF16),
            pltpu.VMEM((group, ny, rows, LANES), BF16),
            pltpu.VMEM((group, *state), BF16),
            pltpu.VMEM((group, nx, *state), BF16),
            pltpu.VMEM((tokens, tokens), F32),
            pltpu.VMEM((heads, tokens), F32),
            pltpu.VMEM((tokens, LANES), F32),
            pltpu.VMEM((heads, tokens), F32),
            pltpu.VMEM((tokens, 2 * states), F32),
            pltpu.VMEM((tokens, 2 * states), BF16),
            pltpu.VMEM((ny, nx, nc, half, states), BF16),
            pltpu.VMEM((ny, nx, nc, half, states), BF16),
            pltpu.VMEM((ny, nx, half, states), BF16),
            pltpu.VMEM((ny, nx, half, states), BF16),
            pltpu.VMEM((ny, nx, half, states), BF16),
            pltpu.VMEM((ny, nx, half, states), BF16),
            pltpu.VMEM((nx, half, states), F32),
            pltpu.VMEM((nx, half, states), F32),
            pltpu.VMEM((ny, nx, half, states), BF16),
            pltpu.VMEM((ny, nx, half, states), BF16),
            pltpu.VMEM((ny, half, states), BF16),
            pltpu.VMEM((ny, half, states), BF16),
            pltpu.VMEM((2, share, final_pad, states), F32),
            pltpu.VMEM((2, nz, final_pad, states), F32),
            pltpu.VMEM((nx, ny, peak_pad), F32),
            pltpu.VMEM((nx, ny, peak_pad), F32),
            pltpu.VMEM((ny, 1, peak_pad), F32),
            pltpu.VMEM((ny, 1, peak_pad), F32),
            pltpu.VMEM((1, peak_pad), F32),
            pltpu.VMEM((ends, 1, peak_pad), F32),
            dma((7,)),
            dma((nx,)), dma((nx,)),
            dma((group, nx)), dma((group, nx)),
            dma((ny,)), dma((ny,)),
            dma((group, ny)), dma((group, ny)),
            dma((group, ny)), dma((group, ny)),
            dma((group, nx)), dma((group, nx)),
            dma, dma,
            dma((ny,)), dma((ny,)),
            dma((ny,)), dma((ny,)),
            dma((nx,)), dma((nx,)),
            dma((ny, nx)), dma((ny, nx)),
            dma((ny,)), dma((ny,)),
            dma((2, share)), dma((2, nz)),
            dma((nx,)), dma((nx,)),
            dma((ny,)), dma((ny,)),
            dma((ends,)), dma((ends,)),
        ],
        compiler_params=pltpu.CompilerParams(
            collective_id=0, has_side_effects=True, vmem_limit_bytes=VMEM_BYTES
        ),
        name="scan",
    )(
        layer_input.reshape(tokens, width),
        scan_input.reshape(tokens, channels),
        scan_cotangent.reshape(tokens, channels),
        step_size.reshape(heads, tokens),
        log_decay.reshape(heads, tokens),
        state_inputs.reshape(tokens, 2 * states),
        entry_state.reshape(channels, states),
    )
    return (sig.reshape(1, tokens, 2 * states), grad)


def arranged(devices, sizes):
    torus = Mesh(devices.reshape(sizes), AXES)
    placed = (
        P(DP, SEQ, None),
        P(DP, SEQ, None),
        P(DP, SEQ, None),
        P(DP, None, SEQ),
        P(DP, None, SEQ),
        P(DP, SEQ, None),
        P(DP, SEQ, None, None),
    )
    return jax.shard_map(
        functools.partial(on_device, sizes),
        mesh=torus,
        in_specs=placed,
        out_specs=(P(DP, SEQ, None), P(AXES, None)),
        check_vma=False,
    )


def solution(mesh):
    return arranged(mesh.devices, (8, 4, 8, 2))
```

time: 80.3 us -> 69 us (0.86)
  Pallas kernels: 76.5 us -> 65.4 us
  local copies, waits for them, and re-layouts: 1.37 us -> 2.86 us
  other arithmetic: 1.45 us -> 0 us
    pallas_call x2 -> x1, Pallas kernels: 76.5 us -> 65.4 us  [on_device(): pl.pallas_call(functools.partial(scan_kernel, sizes), out_shape=(jax.Shap...]
    unnamed x3 -> x2, local copies, waits for them, and re-layouts: 0.66 us -> 2.86 us
    mul x1 -> x0, other arithmetic: 1.37 us -> none  [on_device(): grad = summed[:final] * (1.0 / (own_peaks + EPSILON))[:, None]]
where the time goes in v2:
time: 69 us; the launch traced here: 68.9 us
  Pallas kernels  65.4 us (95%)
  local copies, waits for them, and re-layouts  2.86 us (4%)
    pallas_call x1, Pallas kernels, on_device(): pl.pallas_call(functools.partial(scan_kernel, sizes), out_shape=(jax.Shap...  65.4 us
    unnamed x2, local copies, waits for them, and re-layouts  2.86 us

profile of v2, /device:TPU:1, one launch (start us, length us, event | category | flops | bytes accessed | tf_op | source)
XLA Modules:
  0.0 68.9 jit_solution(4437641410797763608)
XLA Ops:
  0.6 65.4 %scan.1 = (bf16[256,256]{1,0:T(8,128)(2,1)}, f32[5,256]{1,0:T(8,128)}) custom-call(bf16[256,2560]{1,0:T(8,128)(2,1)} %bitcast.8, bf16[256,2560]{1,0:T(8,128)(2,1)} %bitcast.9, bf16[256,2560]{1,0:T(8,128)(2,1)} %bitcast.10, f32[40,256]{1,0:T(8,128)} %bitcast.14, f32[40,256]{1,0:T(8,128)} %bitcast.15, bf16[256,256]{1,0:T(8,128)(2,1)} %bitcast.12, ...), custom_call_target="tpu_custom_call" | custom-call | tf_op jit(solution)/shard_map/scan/pallas_call | solution.py:584
  66.0 1.6 %copy.11 = bf16[1,256,256]{2,1,0:T(8,128)(2,1)} copy(bf16[1,256,256]{2,1,0:T(8,128)(2,1)} %bitcast.13) | data formatting | bytes 262144
  67.6 1.3 %copy.12 = f32[5,256]{1,0:T(8,128)} copy(f32[5,256]{1,0:T(8,128)} %get-tuple-element.9) | data formatting | bytes 10240

commit v3 on v2

--- a/solution.py
+++ b/solution.py
@@ -17,7 +17,7 @@
 EPSILON = 1e-06
 LANES = 128
 FAR = -1.0e9
-VMEM_BYTES = 60 * 1024 * 1024
+VMEM_BYTES = 55200 * 1024
 
 
 def product(a, b):
@@ -37,10 +37,17 @@
     return pieces
 
 
-def one_hot(heads, width, first, head_size):
-    row = lax.broadcasted_iota(jnp.int32, (heads, width), 0)
-    lane = lax.broadcasted_iota(jnp.int32, (heads, width), 1) + first
+def stacked(x, parts):
+    pieces = [piece.astype(F32) for piece in split(x, parts)]
+    return jnp.concatenate(pieces, axis=0).T.astype(BF16)
+
+
+def one_hot(heads, parts, width, first, head_size):
+    row = lax.broadcasted_iota(jnp.int32, (parts * heads, width), 0)
+    lane = lax.broadcasted_iota(jnp.int32, (parts * heads, width), 1) + first
     start = row * head_size
+    for k in range(1, parts):
+        start = jnp.where(row >= k * heads, (row - k * heads) * head_size, start)
     return jnp.where((lane >= start) & (lane < start + head_size), 1.0, 0.0).astype(BF16)
 
 
@@ -58,12 +65,12 @@
 def scan_kernel(
     sizes,
     x_hbm, in_hbm, cot_hbm, step_hbm, ld_hbm, si_hbm, es_hbm,
-    sig_ref, out_ref,
-    xv, inv, cotv, stepv, ldv, siv, esv,
+    sig_hbm, out_ref,
+    sig_ref, xv, inv, cotv, stepv, ldv, siv, esv,
     wc, wi, xt, fl, by, rx1, tot_s, tot_x, tots_y, tot_y, rs, ry1, bs, ry2, bx,
     mm, cum_ref, cs_ref, ei_ref, slope_ref, act_ref,
     gr, gw, pair_r, pair_w, sy, ry, sxr, rxr, sx, rx, s2, r2, sz, rz, px_s, px_r, py_s, py_r, pz_s, pz_r,
-    in_sem, tot_ss, tot_rs, x1_ss, x1_rs, toty_ss, toty_rs, y1_ss, y1_rs, y2_ss, y2_rs, x2_ss, x2_rs,
+    in_sem, sig_sem, tot_ss, tot_rs, x1_ss, x1_rs, toty_ss, toty_rs, y1_ss, y1_rs, y2_ss, y2_rs, x2_ss, x2_rs,
     pr_ss, pr_rs, pw_ss, pw_rs, gy_ss, gy_rs, gx_ss, gx_rs, wx_ss, wx_rs, wy_ss, wy_rs, z_ss, z_rs,
     px_ss, px_rs, py_ss, py_rs, pz_ss, pz_rs,
 ):
@@ -101,13 +108,13 @@
         pltpu.make_async_copy(src, dst, in_sem.at[i])
         for i, (src, dst) in enumerate(
             (
-                (ld_hbm, ldv), (si_hbm, siv), (cot_hbm, cotv), (step_hbm, stepv),
-                (in_hbm, inv), (es_hbm, esv), (x_hbm, xv),
+                (ld_hbm, ldv), (si_hbm, siv), (step_hbm, stepv), (in_hbm, inv), (es_hbm, esv), (x_hbm, xv),
+                (cot_hbm, cotv),
             )
         )
     ]
-    for copy in arrivals:
-        copy.start()
+    for i in (0, 1, 6):
+        arrivals[i].start()
 
     barrier = pltpu.get_barrier_semaphore()
     for d in range(1, nx):
@@ -129,8 +136,7 @@
     last = cum[:, tokens - 1 : tokens]
     cum_ref[...] = cum
     cs_ref[:, 0:heads] = cum.T
-    factor_parts = split(jnp.exp(cum).T, 2)
-    total_parts = split(jnp.broadcast_to(jnp.exp(last), (heads, LANES)).T[0:8, :], 3)
+    factor = stacked(jnp.exp(cum), 3)
     arrivals[1].wait()
     preact = siv[...].astype(F32)
     sigma = 1.0 / (1.0 + jnp.exp(-preact))
@@ -139,22 +145,6 @@
     act_ref[...] = act.astype(BF16)
     reads_t = act[:, states:].T.astype(BF16)
 
-    arrivals[2].wait()
-    for at in range(0, channels, 2 * LANES):
-        hot = one_hot(heads, 2 * LANES, at, head_size)
-        spread = product(factor_parts[0], hot) + product(factor_parts[1], hot)
-        weighted = (cotv[:, at : at + 2 * LANES].astype(F32) * spread).astype(BF16)
-        wc[:, at : at + 2 * LANES] = weighted
-        local = product(reads_t, weighted).astype(BF16)
-        fl[at // LANES] = local[:, :LANES]
-        fl[at // LANES + 1] = local[:, LANES:]
-    for i in range(tiles):
-        hot = one_hot(heads, LANES, i * LANES, head_size)
-        spread = functools.reduce(jnp.add, [product(p, hot) for p in reversed(total_parts)])
-        tot_s[i // group, i % group : i % group + 1, :] = spread[0:1, :]
-
-    pl.semaphore_wait(barrier, nx - 1 + ny - 1 + ends - 1)
-
     def tot_x_copy(d):
         to = beside(d)
         return send(tot_s.at[to], tot_x.at[x], tot_ss.at[d], tot_rs.at[d], {"seq_1": to})
@@ -235,6 +225,21 @@
             def _():
                 rz[side, z] = sz[side, i]
 
+    for i in (2, 3, 4, 5):
+        arrivals[i].start()
+    arrivals[6].wait()
+    for at in range(0, channels, 2 * LANES):
+        hot = one_hot(heads, 3, 2 * LANES, at, head_size)
+        spread = product(factor, hot)
+        for n in range(2):
+            i = at // LANES + n
+            tot_s[i // group, i % group : i % group + 1, :] = spread[tokens - 1 :, n * LANES : (n + 1) * LANES]
+        weighted = (cotv[:, at : at + 2 * LANES].astype(F32) * spread).astype(BF16)
+        wc[:, at : at + 2 * LANES] = weighted
+        local = product(reads_t, weighted).astype(BF16)
+        fl[at // LANES] = local[:, :LANES]
+        fl[at // LANES + 1] = local[:, LANES:]
+    pl.semaphore_wait(barrier, nx - 1 + ny - 1 + ends - 1)
     for d in range(1, nx):
         tot_x_copy(d).start()
     for g in range(group):
@@ -244,9 +249,9 @@
         rx1[g, x] = fl[x * group + g]
     tot_x[x] = tot_s[x]
 
+    arrivals[2].wait()
+    ei_ref[...] = stepv[...] * jnp.exp(last - cum_ref[...])
     arrivals[3].wait()
-    ei_ref[...] = stepv[...] * jnp.exp(last - cum_ref[...])
-    arrivals[4].wait()
     mm[...] = jnp.zeros_like(mm)
     far = jnp.where(
         lax.broadcasted_iota(jnp.int32, (LANES, LANES), 0)
@@ -334,7 +339,7 @@
             x2_copy(g, d).start()
 
     row_part(0)
-    arrivals[5].wait()
+    arrivals[4].wait()
     mixing = mm[...]
     reads = act_ref[:, states:]
     writes = act_ref[:, :states]
@@ -343,7 +348,7 @@
     read_side = (grad_read * slope_ref[:, states:]).astype(BF16)
     sig_ref[:, states:] = read_side
     row_part(1)
-    arrivals[6].wait()
+    arrivals[5].wait()
     eye = jnp.where(
         lax.broadcasted_iota(jnp.int32, (LANES, LANES), 0)
         == lax.broadcasted_iota(jnp.int32, (LANES, LANES), 1),
@@ -356,7 +361,7 @@
 
     def gradient(side_value, store, b):
         block = nx * part
-        value = product(xt[b * block : (b + 1) * block, :], side_value)
+        value = product(xt[pl.ds(pl.multiple_of(b * block, block), block), :], side_value)
         for k in range(nx):
             for h in range(nc):
                 at = k * part + h * half
@@ -372,10 +377,10 @@
     inner_write = product(mixing.T.astype(BF16), reads)
     suffix(1)
 
-    entering_parts = split(ei_ref[...].T, 2)
+    entering = stacked(ei_ref[...], 3)
     for at in range(0, channels, 2 * LANES):
-        hot = one_hot(heads, 2 * LANES, at, head_size)
-        spread = product(entering_parts[0], hot) + product(entering_parts[1], hot)
+        hot = one_hot(heads, 3, 2 * LANES, at, head_size)
+        spread = product(entering, hot)
         wi[:, at : at + 2 * LANES] = (inv[:, at : at + 2 * LANES].astype(F32) * spread).astype(BF16)
     suffix(2)
 
@@ -426,24 +431,8 @@
     for d in range(1, ends):
         pz_copy(d).start()
 
-    for g in range(2):
-        for d in range(1, nx):
-            x2_copy(g, d).wait_recv()
     carried = inner_write
-    for g in range(2):
-        for k in range(nx):
-            i = k * group + g
-            carried = carried + product_nt(wi[:, i * LANES : (i + 1) * LANES], by[i])
-
-    read_sum = gr[y, :, c].astype(F32) + pair_r[y].astype(F32)
-    for d in range(1, ny):
-        gy_copy(d).wait_recv()
-        read_sum = read_sum + ry[d].astype(F32)
-    sxr[...] = read_sum
-    for d in range(1, nx):
-        gx_copy(d).start()
-
-    for g in range(2, group):
+    for g in range(group):
         for d in range(1, nx):
             x2_copy(g, d).wait_recv()
         for k in range(nx):
@@ -456,13 +445,8 @@
         gradient(write_side, gw, b)
     for k in range(ny):
         pair_w_copy(k).start()
-
-    for d in range(1, nx):
-        gx_copy(d).wait_recv()
-    read_sum = sxr[x]
-    for d in range(1, nx):
-        read_sum = read_sum + rxr[d]
-    start_z(1, read_sum)
+    sig_copy = pltpu.make_async_copy(sig_ref, sig_hbm, sig_sem)
+    sig_copy.start()
 
     def first(k, carry):
         pair_w_copy(k).wait_recv()
@@ -475,6 +459,14 @@
 
     lax.fori_loop(0, ny, first, 0)
 
+    read_sum = gr[y, :, c].astype(F32) + pair_r[y].astype(F32)
+    for d in range(1, ny):
+        gy_copy(d).wait_recv()
+        read_sum = read_sum + ry[d].astype(F32)
+    sxr[...] = read_sum
+    for d in range(1, nx):
+        gx_copy(d).start()
+
     def gathered(k):
         to = along(1 + k)
         total = gw[to, x, c].astype(F32) + pair_w[to, x].astype(F32)
@@ -489,6 +481,12 @@
         return carry
 
     lax.fori_loop(0, ny - 1, second, 0)
+    for d in range(1, nx):
+        gx_copy(d).wait_recv()
+    read_sum = sxr[x]
+    for d in range(1, nx):
+        read_sum = read_sum + rxr[d]
+    start_z(1, read_sum)
     total = gathered(ny - 1)
     for k in range(ny - 1):
         wy_copy(k).wait_recv()
@@ -527,6 +525,7 @@
     for d in range(1, ends):
         pz_copy(d).wait_send()
     pair_r_copy().wait_send()
+    sig_copy.wait()
 
     def drain(g, carry):
         for d in range(1, nx):
@@ -588,8 +587,9 @@
             jax.ShapeDtypeStruct((final, 2 * states), F32),
         ),
         in_specs=[anywhere] * 7,
-        out_specs=(vmem, vmem),
+        out_specs=(anywhere, vmem),
         scratch_shapes=[
+            pltpu.VMEM((tokens, 2 * states), BF16),
             pltpu.VMEM((tokens, width), BF16),
             pltpu.VMEM(big, BF16),
             pltpu.VMEM(big, BF16),
@@ -638,7 +638,7 @@
             pltpu.VMEM((ny, 1, peak_pad), F32),
             pltpu.VMEM((1, peak_pad), F32),
             pltpu.VMEM((ends, 1, peak_pad), F32),
-            dma((7,)),
+            dma((7,)), dma,
             dma((nx,)), dma((nx,)),
             dma((group, nx)), dma((group, nx)),
             dma((ny,)), dma((ny,)),

time: 69 us -> 65.1 us (0.943)
  Pallas kernels: 65.4 us -> 62.1 us
    pallas_call x1, Pallas kernels: 65.4 us -> 62.1 us  [on_device(): pl.pallas_call(functools.partial(scan_kernel, sizes), out_shape=(jax.Shap...]
    unnamed x2, local copies, waits for them, and re-layouts: 2.86 us -> 2.17 us
where the time goes in v3:
time: 65.1 us; the launch traced here: 64.9 us
  Pallas kernels  62.1 us (95%)
  local copies, waits for them, and re-layouts  2.17 us (3%)
    pallas_call x1, Pallas kernels, on_device(): pl.pallas_call(functools.partial(scan_kernel, sizes), out_shape=(jax.Shap...  62.1 us
    unnamed x2, local copies, waits for them, and re-layouts  2.17 us

profile of v3, /device:TPU:1, one launch (start us, length us, event | category | flops | bytes accessed | tf_op | source)
XLA Modules:
  0.0 64.9 jit_solution(2667509296712849604)
XLA Ops:
  0.6 62.1 %scan.1 = (bf16[256,256]{1,0:T(8,128)(2,1)}, f32[5,256]{1,0:T(8,128)S(1)}) custom-call(bf16[256,2560]{1,0:T(8,128)(2,1)} %bitcast.8, bf16[256,2560]{1,0:T(8,128)(2,1)} %bitcast.9, bf16[256,2560]{1,0:T(8,128)(2,1)} %bitcast.10, f32[40,256]{1,0:T(8,128)} %bitcast.14, f32[40,256]{1,0:T(8,128)} %bitcast.15, bf16[256,256]{1,0:T(8,128)(2,1)} %bitcast.12, ...), custom_call_target="tpu_custom_call" | custom-call | tf_op jit(solution)/shard_map/scan/pallas_call | solution.py:583
  62.7 1.6 %copy.11 = bf16[1,256,256]{2,1,0:T(8,128)(2,1)} copy(bf16[1,256,256]{2,1,0:T(8,128)(2,1)} %bitcast.13) | data formatting | bytes 262144
  64.3 0.6 copy.12

commit v4 on v3

--- a/solution.py
+++ b/solution.py
@@ -17,7 +17,7 @@
 EPSILON = 1e-06
 LANES = 128
 FAR = -1.0e9
-VMEM_BYTES = 55200 * 1024
+VMEM_BYTES = 48 * 1024 * 1024
 
 
 def product(a, b):
@@ -405,21 +405,23 @@
 
     for g in range(3, group):
         suffix(g)
+    for d in range(1, nx):
+        px_copy(d).wait_recv()
+    top = px_s[x]
+    for d in range(1, nx):
+        top = jnp.maximum(top, px_r[d])
+    for k in range(ny):
+        py_s[k] = top[k : k + 1, :]
+    for d in range(1, ny):
+        py_copy(d).start()
+    expand(0)
+    expand(1)
     pair_r_copy().wait_recv()
     for d in range(1, ny):
         to = along(d)
         sy[d] = (gr[to, :, c].astype(F32) + pair_r[to].astype(F32)).astype(BF16)
         gy_copy(d).start()
-    for d in range(1, nx):
-        px_copy(d).wait_recv()
-    top = px_s[x]
-    for d in range(1, nx):
-        top = jnp.maximum(top, px_r[d])
-    for k in range(ny):
-        py_s[k] = top[k : k + 1, :]
-    for d in range(1, ny):
-        py_copy(d).start()
-    for g in range(group):
+    for g in range(2, group):
         expand(g)
 
     for d in range(1, ny):
@@ -661,13 +663,18 @@
         ),
         name="scan",
     )(
-        layer_input.reshape(tokens, width),
-        scan_input.reshape(tokens, channels),
-        scan_cotangent.reshape(tokens, channels),
-        step_size.reshape(heads, tokens),
-        log_decay.reshape(heads, tokens),
-        state_inputs.reshape(tokens, 2 * states),
-        entry_state.reshape(channels, states),
+        *(
+            pltpu.with_memory_space_constraint(array, pltpu.HBM)
+            for array in (
+                layer_input.reshape(tokens, width),
+                scan_input.reshape(tokens, channels),
+                scan_cotangent.reshape(tokens, channels),
+                step_size.reshape(heads, tokens),
+                log_decay.reshape(heads, tokens),
+                state_inputs.reshape(tokens, 2 * states),
+                entry_state.reshape(channels, states),
+            )
+        )
     )
     return (sig.reshape(1, tokens, 2 * states), grad)
 

time: 65.1 us -> 62.7 us (0.963)
  Pallas kernels: 62.1 us -> 60.6 us
  local copies, waits for them, and re-layouts: 2.17 us -> 1.26 us
    pallas_call x1, Pallas kernels: 62.1 us -> 60.6 us  [on_device(): pl.pallas_call(functools.partial(scan_kernel, sizes), out_shape=(jax.Shap...]
    unnamed x2, local copies, waits for them, and re-layouts: 2.17 us -> 1.26 us
where the time goes in v4:
time: 62.7 us; the launch traced here: 62.5 us
  Pallas kernels  60.6 us (97%)
  local copies, waits for them, and re-layouts  1.26 us (2%)
  between operations  0.64 us (1%)
    pallas_call x1, Pallas kernels, on_device(): pl.pallas_call(functools.partial(scan_kernel, sizes), out_shape=(jax.Shap...  60.6 us
    unnamed x2, local copies, waits for them, and re-layouts  1.26 us

profile of v4, /device:TPU:1, one launch (start us, length us, event | category | flops | bytes accessed | tf_op | source)
XLA Modules:
  0.0 62.5 jit_solution(12311518844722320236)
XLA Ops:
  0.6 60.6 %scan.1 = (bf16[256,256]{1,0:T(8,128)(2,1)S(1)}, f32[5,256]{1,0:T(8,128)S(1)}) custom-call(bf16[256,2560]{1,0:T(8,128)(2,1)} %bitcast.9, bf16[256,2560]{1,0:T(8,128)(2,1)} %bitcast.10, bf16[256,2560]{1,0:T(8,128)(2,1)} %bitcast.11, f32[40,256]{1,0:T(8,128)} %bitcast.14, f32[40,256]{1,0:T(8,128)} %bitcast.15, bf16[256,256]{1,0:T(8,128)(2,1)} %bitcast.13, ...), custom_call_target="tpu_custom_call" | custom-call | tf_op jit(solution)/shard_map/scan/pallas_call | solution.py:585
  61.3 0.7 %copy.11 = bf16[1,256,256]{2,1,0:T(8,128)(2,1)} copy(bf16[1,256,256]{2,1,0:T(8,128)(2,1)S(1)} %bitcast.8) | data formatting | bytes 262144
  61.9 0.6 copy.12

commit v5 on v4

--- a/solution.py
+++ b/solution.py
@@ -101,6 +101,12 @@
     def along(d):
         return lax.rem(y + d, ny)
 
+    def hop(k):
+        k = jnp.int32(k)
+        return ny // 2 + lax.div(k + 1, jnp.int32(2)) * (1 - 2 * lax.rem(k, jnp.int32(2)))
+
+    far_first = sorted(range(1, ny), key=lambda d: -min(d, ny - d))
+
     def place(to):
         return {"dp_0": to // nc, "dp_1": lax.rem(to, nc)}
 
@@ -179,7 +185,7 @@
         return send(gr.at[:, :, other], pair_r, pr_ss, pr_rs, {"dp_1": other})
 
     def pair_w_copy(k):
-        to = along(1 + k)
+        to = along(hop(k))
         return send(gw.at[to, :, other], pair_w.at[to], pw_ss.at[k], pw_rs.at[k], {"dp_1": other})
 
     def gy_copy(d):
@@ -192,7 +198,7 @@
         return send(sx.at[k, d], rx.at[k, d], wx_ss.at[k, d], wx_rs.at[k, d], {"seq_1": beside(d)})
 
     def wy_copy(k):
-        return send(s2.at[k], r2.at[k], wy_ss.at[k], wy_rs.at[k], {"seq_0": along(1 + k)})
+        return send(s2.at[k], r2.at[k], wy_ss.at[k], wy_rs.at[k], {"seq_0": along(hop(k))})
 
     def px_copy(d):
         return send(px_s.at[beside(d)], px_r.at[d], px_ss.at[d], px_rs.at[d], {"seq_1": beside(d)})
@@ -308,7 +314,7 @@
             state = rx1[g, k].astype(F32) + tot_x[k, g : g + 1, :] * state
         rs[g] = state.astype(BF16)
         ry1[g, y] = rs[g, pl.ds(pl.multiple_of(y * rows, rows), rows)]
-        for d in range(1, ny):
+        for d in far_first:
             y1_copy(g, d).start()
 
     def suffix(g):
@@ -323,7 +329,7 @@
             if k:
                 state = ry1[g, k].astype(F32) + tot_y[k, g : g + 1, :] * state
         ry2[g, pl.ds(pl.multiple_of(y * rows, rows), rows)] = bs[g, y]
-        for d in range(1, ny):
+        for d in far_first:
             y2_copy(g, d).start()
 
     def expand(g):
@@ -452,7 +458,7 @@
 
     def first(k, carry):
         pair_w_copy(k).wait_recv()
-        to = along(1 + k)
+        to = along(hop(k))
         for d in range(1, nx):
             at = beside(d)
             sx[k, d] = (gw[to, at, c].astype(F32) + pair_w[to, at].astype(F32)).astype(BF16)
@@ -470,7 +476,7 @@
         gx_copy(d).start()
 
     def gathered(k):
-        to = along(1 + k)
+        to = along(hop(k))
         total = gw[to, x, c].astype(F32) + pair_w[to, x].astype(F32)
         for d in range(1, nx):
             wx_copy(k, d).wait_recv()

time: 62.7 us -> 61.4 us (0.979)
  Pallas kernels: 60.6 us -> 59.4 us
    pallas_call x1, Pallas kernels: 60.6 us -> 59.4 us  [on_device(): pl.pallas_call(functools.partial(scan_kernel, sizes), out_shape=(jax.Shap...]
where the time goes in v5:
time: 61.4 us; the launch traced here: 61.3 us
  Pallas kernels  59.4 us (97%)
  local copies, waits for them, and re-layouts  1.26 us (2%)
  between operations  0.64 us (1%)
    pallas_call x1, Pallas kernels, on_device(): pl.pallas_call(functools.partial(scan_kernel, sizes), out_shape=(jax.Shap...  59.4 us
    unnamed x2, local copies, waits for them, and re-layouts  1.26 us

profile of v5, /device:TPU:1, one launch (start us, length us, event | category | flops | bytes accessed | tf_op | source)
XLA Modules:
  0.0 61.3 jit_solution(2751085094021801777)
XLA Ops:
  0.6 59.4 %scan.1 = (bf16[256,256]{1,0:T(8,128)(2,1)S(1)}, f32[5,256]{1,0:T(8,128)S(1)}) custom-call(bf16[256,2560]{1,0:T(8,128)(2,1)} %bitcast.9, bf16[256,2560]{1,0:T(8,128)(2,1)} %bitcast.10, bf16[256,2560]{1,0:T(8,128)(2,1)} %bitcast.11, f32[40,256]{1,0:T(8,128)} %bitcast.14, f32[40,256]{1,0:T(8,128)} %bitcast.15, bf16[256,256]{1,0:T(8,128)(2,1)} %bitcast.13, ...), custom_call_target="tpu_custom_call" | custom-call | tf_op jit(solution)/shard_map/scan/pallas_call | solution.py:591
  60.0 0.7 %copy.11 = bf16[1,256,256]{2,1,0:T(8,128)(2,1)} copy(bf16[1,256,256]{2,1,0:T(8,128)(2,1)S(1)} %bitcast.8) | data formatting | bytes 262144
  60.7 0.6 copy.12
